TPU v7x, 16 devices: a whole 2x2x2 slice. The times are simulated.
16 devices in a mesh: dp: 2 (over z), sp: 8 (over y, x, core).
Axes of the slice: x: 2, y: 2, z: 2, core: 2. Of those that a mesh axis runs over, the one named last changes fastest.
Arguments:
- x: bfloat16 [4, 4096], P('dp'), parts along dimension 0
- wq: bfloat16 [4096, 4096], replicated
- wk: bfloat16 [4096, 1024], replicated
- wv: bfloat16 [4096, 1024], replicated
- wo: bfloat16 [4096, 4096], P('sp')
- kc: bfloat16 [4, 32768, 8, 128], P('dp', 'sp'), parts along dimension 0
- vc: bfloat16 [4, 32768, 8, 128], P('dp', 'sp'), parts along dimension 0
- pos: int32 [4], P('dp'), parts along dimension 0
- lens: int32 [4], P('dp'), parts along dimension 0
Outputs:
- output 1: bfloat16 [4, 4096], P('dp'), parts along dimension 0
- output 2: bfloat16 [4, 32768, 8, 128], P('dp', 'sp'), parts along dimension 0
- output 3: bfloat16 [4, 32768, 8, 128], P('dp', 'sp'), parts along dimension 0
There are 2 independent parts. A program takes and returns all parts, laid end to end along the dimension named above; an argument that names none is the same for every part.
All inputs are finite; a program needn't handle non-finite values.
Results may differ from a plain program's by a relative error of at most 0.00351591.
Values are sent between devices in bfloat16 or wider.
A program may use at most 1 GiB of HBM per device.

v0:
```python
import functools

import jax
import jax.numpy as jnp
from jax import lax
from jax.experimental import pallas as pl
from jax.experimental.pallas import tpu as pltpu
from jax.sharding import PartitionSpec as P

MESH = pl.DeviceIdType.MESH
ANY = pl.BlockSpec(memory_space=pl.ANY)
VMEM = pl.BlockSpec(memory_space=pltpu.VMEM)
SMEM = pl.BlockSpec(memory_space=pltpu.SMEM)
f32 = jnp.float32
bf16 = jnp.bfloat16
LOG2E = 1.4426950408889634
MIB = 1 << 20


def greet(n):
    me = lax.axis_index('sp')
    barrier = pltpu.get_barrier_semaphore()
    for d in range(1, n):
        pl.semaphore_signal(barrier, inc=1, device_id={'sp': lax.rem(me + d, n)}, device_id_type=MESH)


def awaited(n):
    pl.semaphore_wait(pltpu.get_barrier_semaphore(), n - 1)


def lookup(n, wch, ch, slabs, early, pos, lens, x, wq, wk, wv, kc, vc, gat_out, kbuf, vbuf, sc, mrun, snew,
           xb, wqb, wkb, wvb, send, gat, qbd, xsem, wsem, ksem, vsem, ssem, rsem):
    me = lax.axis_index('sp')
    nb, dm = xb.shape
    dq, dh = wqb.shape[1], wkb.shape[1]
    rows = dm // wch
    g = dq // dh
    nkv = n
    npos = kbuf.shape[1] // nkv
    nch = npos // ch
    total = nb * nch
    crow = ch * nkv
    srow = crow // slabs
    heads = 128 // slabs
    start = me * npos
    ninf = -jnp.inf

    def chunk(i):
        return i // nch, pl.ds(pl.multiple_of(i % nch * crow, crow), crow)

    def read_k(i):
        b, r = chunk(i)
        return pltpu.make_async_copy(kc.at[b, r], kbuf.at[b, r], ksem.at[i])

    def read_v(i):
        b, r = chunk(i)
        return pltpu.make_async_copy(vc.at[b, r], vbuf.at[b, r], vsem.at[i])

    xcp = pltpu.make_async_copy(x, xb, xsem)
    xcp.start()
    cps = []
    for c in range(wch):
        r = pl.ds(c * rows, rows)
        trio = []
        for j, (w, buf, cols) in enumerate(((wq, wqb, dq), (wk, wkb, dh), (wv, wvb, dh))):
            cp = pltpu.make_async_copy(w.at[r, pl.ds(pl.multiple_of(me * cols, 128), cols)], buf.at[r], wsem.at[j, c])
            cp.start()
            trio.append(cp)
        cps.append(trio)
    greet(n)
    xcp.wait()
    aq = jnp.zeros((nb, dq), f32)
    ak = jnp.zeros((nb, dh), f32)
    av = jnp.zeros((nb, dh), f32)
    for c in range(wch):
        for cp in cps[c]:
            cp.wait()
        for i in range(c * total // wch, (c + 1) * total // wch):
            read_k(i).start()
        xc = xb[:, c * rows:(c + 1) * rows]
        r = pl.ds(c * rows, rows)
        aq += jnp.dot(xc, wqb[r, :], preferred_element_type=f32)
        ak += jnp.dot(xc, wkb[r, :], preferred_element_type=f32)
        av += jnp.dot(xc, wvb[r, :], preferred_element_type=f32)
    for b in range(nb):
        pieces = [aq[b:b + 1, i * dh:(i + 1) * dh] for i in range(g)] + [ak[b:b + 1], av[b:b + 1]]
        pieces.append(jnp.zeros((8 - g - 2, dh), f32))
        tile = jnp.concatenate(pieces, axis=0).astype(bf16)
        send[b] = tile
        gat[me, b] = tile
    for i in range(early):
        read_v(i).start()
    awaited(n)
    out = []
    for d in range(1, n):
        cp = pltpu.make_async_remote_copy(
            src_ref=send, dst_ref=gat.at[me], send_sem=ssem.at[d], recv_sem=rsem.at[d],
            device_id={'sp': lax.rem(me + d, n)}, device_id_type=MESH)
        cp.start()
        out.append(cp)
    for cp in out:
        cp.wait()

    gat_out[...] = gat[...]
    gf = gat[...].astype(f32)
    sub = lax.broadcasted_iota(jnp.int32, (nkv, 128), 0)
    lane = lax.broadcasted_iota(jnp.int32, (nkv, 128), 1)
    own = sub == (lane % heads) // g
    first = jnp.where(own, lane // heads * (ch // slabs), 1 << 29)
    for b in range(nb):
        q = jnp.concatenate([gf[i, b, 0:g] for i in range(nkv)], axis=0)
        kn = jnp.concatenate([gf[i, b, g:g + 1] for i in range(nkv)], axis=0)
        zero = jnp.zeros_like(q)
        for s in range(slabs):
            a = jnp.concatenate([q if i == s else zero for i in range(slabs)], axis=0)
            qbd[b, s * dh:(s + 1) * dh, :] = a.T.astype(bf16)
        k16 = jnp.concatenate([kn, jnp.zeros_like(kn)], axis=0).astype(bf16)
        t = jnp.dot(k16, qbd[b, 0:dh, :], preferred_element_type=f32)[0:nkv]
        here = jnp.logical_and(pos[b] >= start, pos[b] < jnp.minimum(start + npos, lens[b]))
        limit = jnp.where(here, heads, 0)
        t = jnp.where(jnp.logical_and(own, lane < limit), t, ninf)
        snew[b] = t
        mrun[b] = t

    def scores(i, _):
        b, c = i // nch, i % nch
        read_k(i).wait()

        @pl.when(i + early < total)
        def _():
            read_v(i + early).start()

        lim = jnp.minimum(pos[b], lens[b]) - start - c * ch
        acc = None
        for s in range(0, slabs, 2):
            k2 = jnp.concatenate(
                [kbuf[b, pl.ds(pl.multiple_of(c * crow + (s + t) * srow, srow), srow), :] for t in range(2)], axis=1)
            t = jnp.dot(k2, qbd[b, s * dh:(s + 2) * dh, :], preferred_element_type=f32)
            acc = t if acc is None else acc + t
        acc = acc.reshape(srow // nkv, nkv, 128)
        left = lim - lax.broadcasted_iota(jnp.int32, acc.shape, 0)
        t = jnp.where(first[None] < left, acc, ninf)
        sc[b, pl.ds(pl.multiple_of(c * srow, srow), srow), :] = t.reshape(srow, 128)
        mrun[b] = jnp.maximum(mrun[b], t.max(0))
        return 0

    lax.fori_loop(0, total, scores, 0)

    def landed(i, _):
        read_v(i).wait()
        return 0

    lax.fori_loop(0, total, landed, 0)


def attend(ch, slabs, pos, lens, gat, kbuf, vbuf, sc, mrun, snew, part, ko, vo, mall, lrun, orun, knew, vnew,
           ksem, vsem, nsem):
    me = lax.axis_index('sp')
    nkv, nb, _, dh = gat.shape
    npos = kbuf.shape[1] // nkv
    nch = npos // ch
    total = nb * nch
    crow = ch * nkv
    srow = crow // slabs
    heads = 128 // slabs
    g = heads // nkv
    start = me * npos
    scale = dh ** -0.5 * LOG2E
    ninf = -jnp.inf

    def writes(i):
        b, r = i // nch, pl.ds(pl.multiple_of(i % nch * crow, crow), crow)
        return (pltpu.make_async_copy(kbuf.at[b, r], ko.at[b, r], ksem.at[i]),
                pltpu.make_async_copy(vbuf.at[b, r], vo.at[b, r], vsem.at[i]))

    def begin(i, _):
        for cp in writes(i):
            cp.start()
        return 0

    lax.fori_loop(0, total, begin, 0)

    gf = gat[...].astype(f32)
    lrun[...] = jnp.zeros_like(lrun)
    orun[...] = jnp.zeros_like(orun)
    for b in range(nb):
        knew[b] = jnp.concatenate([gf[i, b, g:g + 1] for i in range(nkv)], axis=0).astype(bf16)
        vnew[b] = jnp.concatenate([gf[i, b, g + 1:g + 2] for i in range(nkv)], axis=0).astype(bf16)
        m = jnp.broadcast_to(mrun[b].max(0, keepdims=True), (nkv, 128))
        k = heads
        while k < 128:
            m = jnp.maximum(m, pltpu.roll(m, k, 1))
            k *= 2
        mall[b] = m

    def mix(i, _):
        b, c = i // nch, i % nch
        lim = jnp.minimum(pos[b], lens[b]) - start - c * ch

        @pl.when(lim > 0)
        def _():
            m = mall[b]
            m = jnp.where(m == ninf, 0.0, m)
            t = sc[b, pl.ds(pl.multiple_of(c * srow, srow), srow), :].reshape(srow // nkv, nkv, 128)
            e = jnp.exp2((t - m[None]) * scale)
            lrun[b] += e.sum(0)
            et = e.reshape(srow, 128).astype(bf16).T
            o = orun[b]
            for s in range(slabs):
                v = vbuf[b, pl.ds(pl.multiple_of(c * crow + s * srow, srow), srow), :]
                o += jnp.dot(et[s * heads:(s + 1) * heads], v, preferred_element_type=f32)
            orun[b] = o

        return 0

    lax.fori_loop(0, total, mix, 0)

    half = lax.broadcasted_iota(jnp.int32, (heads, 128), 1) < 64
    for b in range(nb):
        m = mall[b]
        e = jnp.exp2((snew[b] - jnp.where(m == ninf, 0.0, m)) * scale)
        pad = jnp.zeros_like(e)
        e16 = jnp.concatenate([e, pad], axis=0).astype(bf16)
        v16 = jnp.concatenate([vnew[b].astype(f32), pad], axis=0).astype(bf16)
        o = orun[b] + lax.dot_general(e16, v16, (((0,), (0,)), ((), ())), preferred_element_type=f32)[0:heads]
        l = jnp.broadcast_to((lrun[b] + e).sum(0, keepdims=True), (nkv, 128))
        k = heads
        while k < 128:
            l = l + pltpu.roll(l, k, 1)
            k *= 2
        lt = jnp.broadcast_to(l[0:1], (128, 128)).T[0:heads]
        mt = jnp.broadcast_to(m[0:1] * scale, (128, 128)).T[0:heads]
        ml = jnp.where(half, mt, lt)
        for i in range(nkv):
            part[i, 0, b * g:(b + 1) * g, :] = o[i * g:(i + 1) * g, :]
            part[i, 1, b * g:(b + 1) * g, :] = ml[i * g:(i + 1) * g, :]

    def written(i, _):
        for cp in writes(i):
            cp.wait()
        return 0

    lax.fori_loop(0, total, written, 0)
    for b in range(nb):
        p = pos[b] - start

        @pl.when(jnp.logical_and(p >= 0, p < npos))
        def _():
            r = pl.ds(pl.multiple_of(p * nkv, nkv), nkv)
            cps = (pltpu.make_async_copy(knew.at[b], ko.at[b, r], nsem.at[0]),
                   pltpu.make_async_copy(vnew.at[b], vo.at[b, r], nsem.at[1]))
            for cp in cps:
                cp.start()
            for cp in cps:
                cp.wait()


def combine(n, nb, ych, part, wo, y, wob, rbuf, xs, ybuf, wsem, ssem, rsem, ysem, zsem):
    me = lax.axis_index('sp')
    cols = wo.shape[1] // ych
    cps = []
    for c in range(ych):
        cp = pltpu.make_async_copy(wo.at[:, pl.ds(c * cols, cols)], wob.at[c], wsem.at[c])
        cp.start()
        cps.append(cp)
    greet(n)
    awaited(n)
    out = []
    for d in range(1, n):
        peer = lax.rem(me + d, n)
        cp = pltpu.make_async_remote_copy(
            src_ref=part.at[peer], dst_ref=rbuf.at[me], send_sem=ssem.at[d], recv_sem=rsem.at[d],
            device_id={'sp': peer}, device_id_type=MESH)
        cp.start()
        out.append(cp)
    rbuf[me] = part[me]
    for cp in out:
        cp.wait()
    o = rbuf[:, 0]
    ml = rbuf[:, 1]
    m = jnp.broadcast_to(ml[:, :, 0:1], o.shape)
    l = jnp.broadcast_to(ml[:, :, 64:65], o.shape)
    a = jnp.exp2(m - m.max(0)[None])
    out8 = (a * o).sum(0) / (a * l).sum(0)
    g = out8.shape[0] // nb
    dh = out8.shape[1]
    xs[...] = jnp.zeros_like(xs)
    for b in range(nb):
        for j in range(g):
            xs[b:b + 1, j * dh:(j + 1) * dh] = out8[b * g + j:b * g + j + 1]
    xl = xs[...].astype(bf16)
    sent = []
    for c in range(ych):
        cps[c].wait()
        ybuf[me, c] = jnp.dot(xl, wob[c], preferred_element_type=f32)[0:nb]
        for d in range(1, n):
            cp = pltpu.make_async_remote_copy(
                src_ref=ybuf.at[me, c], dst_ref=ybuf.at[me, c], send_sem=ysem.at[c, d], recv_sem=zsem.at[c, d],
                device_id={'sp': lax.rem(me + d, n)}, device_id_type=MESH)
            cp.start()
            sent.append(cp)
    for cp in sent:
        cp.wait()
    for c in range(ych):
        t = ybuf[0, c]
        for i in range(1, n):
            t = t + ybuf[i, c]
        y[:, c * cols:(c + 1) * cols] = t.astype(bf16)


def solution(mesh):
    n = mesh.shape['sp']

    def local(x, wq, wk, wv, wo, kc, vc, pos, lens):
        nb, npos, nkv, dh = kc.shape
        dm = x.shape[1]
        dq = wq.shape[1] // n
        dma = pltpu.SemaphoreType.DMA
        kc = kc.reshape(nb, npos * nkv, dh)
        vc = vc.reshape(nb, npos * nkv, dh)
        wch, ch, slabs, early = 8, 512, 4, 8
        nch = npos // ch
        small = jax.ShapeDtypeStruct((nb, nkv, 128), f32)
        gat, kbuf, vbuf, sc, mrun, snew = pl.pallas_call(
            functools.partial(lookup, n, wch, ch, slabs, early),
            name='lookup',
            out_shape=(jax.ShapeDtypeStruct((n, nb, 8, dh), bf16), pltpu.VMEM(kc.shape, bf16), pltpu.VMEM(vc.shape, bf16),
                       pltpu.VMEM((nb, npos * nkv // slabs, 128), f32), small, small),
            in_specs=[SMEM, SMEM] + [ANY] * 6,
            out_specs=(VMEM,) * 6,
            scratch_shapes=[
                pltpu.VMEM(x.shape, bf16), pltpu.VMEM((dm, dq), bf16), pltpu.VMEM((dm, dh), bf16), pltpu.VMEM((dm, dh), bf16),
                pltpu.VMEM((nb, 8, dh), bf16), pltpu.VMEM((n, nb, 8, dh), bf16), pltpu.VMEM((nb, slabs * dh, 128), bf16),
                dma, dma((3, wch)), dma((nb * nch,)), dma((nb * nch,)), dma((n,)), dma((n,))],
            compiler_params=pltpu.CompilerParams(collective_id=0, has_side_effects=True, vmem_limit_bytes=12 * MIB),
        )(pos, lens, *(pltpu.with_memory_space_constraint(t, pltpu.HBM) for t in (x, wq, wk, wv, kc, vc)))

        part, ko, vo = pl.pallas_call(
            functools.partial(attend, ch, slabs),
            name='attend',
            out_shape=(jax.ShapeDtypeStruct((n, 2, 8, dh), f32), pltpu.HBM(kc.shape, bf16), pltpu.HBM(vc.shape, bf16)),
            in_specs=[SMEM, SMEM] + [VMEM] * 6,
            out_specs=(VMEM, ANY, ANY),
            scratch_shapes=[
                pltpu.VMEM((nb, nkv, 128), f32), pltpu.VMEM((nb, nkv, 128), f32), pltpu.VMEM((nb, 128 // slabs, dh), f32),
                pltpu.VMEM((nb, nkv, dh), bf16), pltpu.VMEM((nb, nkv, dh), bf16),
                dma((nb * nch,)), dma((nb * nch,)), dma((2,))],
            compiler_params=pltpu.CompilerParams(vmem_limit_bytes=12 * MIB),
        )(pos, lens, gat, kbuf, vbuf, sc, mrun, snew)

        ych = 4
        cols = wo.shape[1] // ych
        y = pl.pallas_call(
            functools.partial(combine, n, nb, ych),
            name='combine',
            out_shape=jax.ShapeDtypeStruct((nb, wo.shape[1]), bf16),
            in_specs=[VMEM, ANY],
            out_specs=VMEM,
            scratch_shapes=[
                pltpu.VMEM((ych, wo.shape[0], cols), bf16), pltpu.VMEM((n, 2, 8, dh), f32), pltpu.VMEM((8, wo.shape[0]), f32),
                pltpu.VMEM((n, ych, nb, cols), f32),
                dma((ych,)), dma((n,)), dma((n,)), dma((ych, n)), dma((ych, n))],
            compiler_params=pltpu.CompilerParams(collective_id=1, has_side_effects=True, vmem_limit_bytes=8 * MIB),
        )(part, pltpu.with_memory_space_constraint(wo, pltpu.HBM))
        shape = (nb, npos, nkv, dh)
        return y, ko.reshape(shape), vo.reshape(shape)

    cache = P('dp', 'sp', None, None)
    return jax.shard_map(
        local, mesh=mesh,
        in_specs=(P('dp', None), P(None, None), P(None, None), P(None, None), P('sp', None),
                  cache, cache, P('dp'), P('dp')),
        out_specs=(P('dp', None), cache, cache),
        check_vma=False)
```

profile of v0, /device:TPU:0, one launch (start us, length us, event | category | flops | bytes accessed | tf_op | source)
XLA Modules:
  0.0 43.8 jit_solution(18111476967129239411)
XLA Ops:
  0.6 0.0 copy-start
  0.6 0.6 %copy-done = s32[2]{0:T(128)S(1)} copy-done((s32[2]{0:T(128)S(1)}, s32[2]{0:T(128)}, u32[]{:S(2)}) %copy-start) | copy-done | bytes 32
  1.3 0.0 copy-start.1
  1.3 0.7 %copy-done.1 = s32[2]{0:T(128)S(1)} copy-done((s32[2]{0:T(128)S(1)}, s32[2]{0:T(128)}, u32[]{:S(2)}) %copy-start.1) | copy-done | bytes 32
  1.9 18.7 %lookup.1 = (bf16[8,2,8,128]{3,2,1,0:T(8,128)(2,1)S(1)}, bf16[2,32768,128]{2,1,0:T(8,128)(2,1)S(1)}, bf16[2,32768,128]{2,1,0:T(8,128)(2,1)S(1)}, f32[2,8192,128]...) custom-call(s32[2]{0:T(128)S(1)} %copy-done, s32[2]{0:T(128)S(1)} %copy-done.1, ...), custom_call_target="tpu_custom_call" | custom-call | tf_op jit(solution)/shard_map/lookup/pallas_call | solution.py:324
  20.7 12.3 %attend.1 = (f32[8,2,8,128]{3,2,1,0:T(8,128)S(1)}, bf16[2,32768,128]{2,1,0:T(8,128)(2,1)}, bf16[2,32768,128]{2,1,0:T(8,128)(2,1)}) custom-call(s32[2]{0:T(128)S(1)} %copy-done, s32[2]{0:T(128)S(1)} %copy-done.1, bf16[8,2,8,128]{3,2,1,0:T(8,128)(2,1)S(1)} %get-tuple-element.12.gat, bf16[2,32768,128]{2,1,0:T(8,128)(2,1)S(1)} %get-tuple-element.13.kbuf, ...), custom_call_target="tpu_custom_call" | custom-call | tf_op jit(solution)/shard_map/attend/pallas_call | solution.py:338
  33.0 10.2 %combine.1 = bf16[2,4096]{1,0:T(2,128)(2,1)S(1)} custom-call(f32[8,2,8,128]{3,2,1,0:T(8,128)S(1)} %get-tuple-element.18.part, bf16[512,4096]{1,0:T(8,128)(2,1)} %wo.1), custom_call_target="tpu_custom_call" | custom-call | tf_op jit(solution)/shard_map/combine/pallas_call | solution.py:353
  43.1 0.6 %copy.13 = bf16[2,4096]{1,0:T(2,128)(2,1)} copy(bf16[2,4096]{1,0:T(2,128)(2,1)S(1)} %combine.1) | data formatting | bytes 32768
Async XLA Ops:
  0.6 0.7 %copy-start = (s32[2]{0:T(128)S(1)}, s32[2]{0:T(128)}, u32[]{:S(2)}) copy-start(s32[2]{0:T(128)} %pos.3) | copy-start | bytes 28
  1.3 0.7 %copy-start.1 = (s32[2]{0:T(128)S(1)}, s32[2]{0:T(128)}, u32[]{:S(2)}) copy-start(s32[2]{0:T(128)} %lens.3) | copy-start | bytes 28
where the time goes:
time: 43.9 us; the launch traced here: 43.8 us
  Pallas kernels  41.2 us (94%)
  local copies, waits for them, and re-layouts  1.91 us (4%)
  between operations  0.67 us (2%)
    pallas_call x1, Pallas kernels, local(): pl.pallas_call(functools.partial(lookup, n, wch, ch, slabs, early), name=...  18.7 us
    pallas_call x1, Pallas kernels, local(): pl.pallas_call(functools.partial(attend, ch, slabs), name='attend', out_s...  12.3 us
    pallas_call x1, Pallas kernels, local(): pl.pallas_call(functools.partial(combine, n, nb, ych), name='combine', ou...  10.2 us
    unnamed x5, local copies, waits for them, and re-layouts  1.91 us

commit v1 on v0

--- a/solution.py
+++ b/solution.py
@@ -28,8 +28,8 @@
     pl.semaphore_wait(pltpu.get_barrier_semaphore(), n - 1)
 
 
-def lookup(n, wch, ch, slabs, early, pos, lens, x, wq, wk, wv, kc, vc, gat_out, kbuf, vbuf, sc, mrun, snew,
-           xb, wqb, wkb, wvb, send, gat, qbd, xsem, wsem, ksem, vsem, ssem, rsem):
+def lookup(n, wch, ch, wide, slabs, early, pos_hbm, lens_hbm, x, wq, wk, wv, kc, vc, gat_out, kbuf, vbuf, sc, mrun, snew,
+           pos, lens, xb, wqb, wkb, wvb, send, gat, qbd, isem, xsem, wsem, ksem, vsem, ssem, rsem):
     me = lax.axis_index('sp')
     nb, dm = xb.shape
     dq, dh = wqb.shape[1], wkb.shape[1]
@@ -58,6 +58,9 @@
 
     xcp = pltpu.make_async_copy(x, xb, xsem)
     xcp.start()
+    icps = [pltpu.make_async_copy(pos_hbm, pos, isem.at[0]), pltpu.make_async_copy(lens_hbm, lens, isem.at[1])]
+    for cp in icps:
+        cp.start()
     cps = []
     for c in range(wch):
         r = pl.ds(c * rows, rows)
@@ -101,12 +104,17 @@
     for cp in out:
         cp.wait()
 
+    for cp in icps:
+        cp.wait()
     gat_out[...] = gat[...]
     gf = gat[...].astype(f32)
     sub = lax.broadcasted_iota(jnp.int32, (nkv, 128), 0)
     lane = lax.broadcasted_iota(jnp.int32, (nkv, 128), 1)
     own = sub == (lane % heads) // g
-    first = jnp.where(own, lane // heads * (ch // slabs), 1 << 29)
+    wrow = wide * nkv // slabs
+    wch_n = npos // wide
+    per = wide // ch
+    first = jnp.where(own, lane // heads * (wide // slabs), 1 << 29)
     for b in range(nb):
         q = jnp.concatenate([gf[i, b, 0:g] for i in range(nkv)], axis=0)
         kn = jnp.concatenate([gf[i, b, g:g + 1] for i in range(nkv)], axis=0)
@@ -123,28 +131,30 @@
         mrun[b] = t
 
     def scores(i, _):
-        b, c = i // nch, i % nch
-        read_k(i).wait()
-
-        @pl.when(i + early < total)
+        b, c = i // wch_n, i % wch_n
+        for t in range(per):
+            read_k(i * per + t).wait()
+
+        @pl.when(i * per + early < total)
         def _():
-            read_v(i + early).start()
-
-        lim = jnp.minimum(pos[b], lens[b]) - start - c * ch
+            for t in range(per):
+                read_v(i * per + t + early).start()
+
+        lim = jnp.minimum(pos[b], lens[b]) - start - c * wide
         acc = None
         for s in range(0, slabs, 2):
             k2 = jnp.concatenate(
-                [kbuf[b, pl.ds(pl.multiple_of(c * crow + (s + t) * srow, srow), srow), :] for t in range(2)], axis=1)
+                [kbuf[b, pl.ds(pl.multiple_of((c * slabs + s + t) * wrow, wrow), wrow), :] for t in range(2)], axis=1)
             t = jnp.dot(k2, qbd[b, s * dh:(s + 2) * dh, :], preferred_element_type=f32)
             acc = t if acc is None else acc + t
-        acc = acc.reshape(srow // nkv, nkv, 128)
+        acc = acc.reshape(wrow // nkv, nkv, 128)
         left = lim - lax.broadcasted_iota(jnp.int32, acc.shape, 0)
         t = jnp.where(first[None] < left, acc, ninf)
-        sc[b, pl.ds(pl.multiple_of(c * srow, srow), srow), :] = t.reshape(srow, 128)
+        sc[b, pl.ds(pl.multiple_of(c * wrow, wrow), wrow), :] = t.reshape(wrow, 128)
         mrun[b] = jnp.maximum(mrun[b], t.max(0))
         return 0
 
-    lax.fori_loop(0, total, scores, 0)
+    lax.fori_loop(0, nb * wch_n, scores, 0)
 
     def landed(i, _):
         read_v(i).wait()
@@ -153,8 +163,8 @@
     lax.fori_loop(0, total, landed, 0)
 
 
-def attend(ch, slabs, pos, lens, gat, kbuf, vbuf, sc, mrun, snew, part, ko, vo, mall, lrun, orun, knew, vnew,
-           ksem, vsem, nsem):
+def attend(ch, wide, slabs, pos_hbm, lens_hbm, gat, kbuf, vbuf, sc, mrun, snew, part, ko, vo, pos, lens, mall, lrun, orun, knew, vnew,
+           isem, ksem, vsem, nsem):
     me = lax.axis_index('sp')
     nkv, nb, _, dh = gat.shape
     npos = kbuf.shape[1] // nkv
@@ -168,6 +178,10 @@
     scale = dh ** -0.5 * LOG2E
     ninf = -jnp.inf
 
+    icps = [pltpu.make_async_copy(pos_hbm, pos, isem.at[0]), pltpu.make_async_copy(lens_hbm, lens, isem.at[1])]
+    for cp in icps:
+        cp.start()
+
     def writes(i):
         b, r = i // nch, pl.ds(pl.multiple_of(i % nch * crow, crow), crow)
         return (pltpu.make_async_copy(kbuf.at[b, r], ko.at[b, r], ksem.at[i]),
@@ -193,27 +207,32 @@
             k *= 2
         mall[b] = m
 
+    wrow = wide * nkv // slabs
+    wch_n = npos // wide
+
     def mix(i, _):
-        b, c = i // nch, i % nch
-        lim = jnp.minimum(pos[b], lens[b]) - start - c * ch
+        b, c = i // wch_n, i % wch_n
+        lim = jnp.minimum(pos[b], lens[b]) - start - c * wide
 
         @pl.when(lim > 0)
         def _():
             m = mall[b]
             m = jnp.where(m == ninf, 0.0, m)
-            t = sc[b, pl.ds(pl.multiple_of(c * srow, srow), srow), :].reshape(srow // nkv, nkv, 128)
+            t = sc[b, pl.ds(pl.multiple_of(c * wrow, wrow), wrow), :].reshape(wrow // nkv, nkv, 128)
             e = jnp.exp2((t - m[None]) * scale)
             lrun[b] += e.sum(0)
-            et = e.reshape(srow, 128).astype(bf16).T
+            et = e.reshape(wrow, 128).astype(bf16).T
             o = orun[b]
             for s in range(slabs):
-                v = vbuf[b, pl.ds(pl.multiple_of(c * crow + s * srow, srow), srow), :]
+                v = vbuf[b, pl.ds(pl.multiple_of((c * slabs + s) * wrow, wrow), wrow), :]
                 o += jnp.dot(et[s * heads:(s + 1) * heads], v, preferred_element_type=f32)
             orun[b] = o
 
         return 0
 
-    lax.fori_loop(0, total, mix, 0)
+    for cp in icps:
+        cp.wait()
+    lax.fori_loop(0, nb * wch_n, mix, 0)
 
     half = lax.broadcasted_iota(jnp.int32, (heads, 128), 1) < 64
     for b in range(nb):
@@ -235,9 +254,22 @@
             part[i, 0, b * g:(b + 1) * g, :] = o[i * g:(i + 1) * g, :]
             part[i, 1, b * g:(b + 1) * g, :] = ml[i * g:(i + 1) * g, :]
 
+    def rows(b):
+        r = pl.ds(pl.multiple_of((pos[b] - start) * nkv, nkv), nkv)
+        return (pltpu.make_async_copy(knew.at[b], ko.at[b, r], nsem.at[b, 0]),
+                pltpu.make_async_copy(vnew.at[b], vo.at[b, r], nsem.at[b, 1]))
+
     def written(i, _):
         for cp in writes(i):
             cp.wait()
+        b = i // nch
+        p = pos[b] - start - i % nch * ch
+
+        @pl.when(jnp.logical_and(p >= 0, p < ch))
+        def _():
+            for cp in rows(b):
+                cp.start()
+
         return 0
 
     lax.fori_loop(0, total, written, 0)
@@ -246,12 +278,7 @@
 
         @pl.when(jnp.logical_and(p >= 0, p < npos))
         def _():
-            r = pl.ds(pl.multiple_of(p * nkv, nkv), nkv)
-            cps = (pltpu.make_async_copy(knew.at[b], ko.at[b, r], nsem.at[0]),
-                   pltpu.make_async_copy(vnew.at[b], vo.at[b, r], nsem.at[1]))
-            for cp in cps:
-                cp.start()
-            for cp in cps:
+            for cp in rows(b):
                 cp.wait()
 
 
@@ -318,35 +345,37 @@
         dma = pltpu.SemaphoreType.DMA
         kc = kc.reshape(nb, npos * nkv, dh)
         vc = vc.reshape(nb, npos * nkv, dh)
-        wch, ch, slabs, early = 8, 512, 4, 8
+        wch, ch, wide, slabs, early = 8, 512, 1024, 4, 8
         nch = npos // ch
         small = jax.ShapeDtypeStruct((nb, nkv, 128), f32)
         gat, kbuf, vbuf, sc, mrun, snew = pl.pallas_call(
-            functools.partial(lookup, n, wch, ch, slabs, early),
+            functools.partial(lookup, n, wch, ch, wide, slabs, early),
             name='lookup',
             out_shape=(jax.ShapeDtypeStruct((n, nb, 8, dh), bf16), pltpu.VMEM(kc.shape, bf16), pltpu.VMEM(vc.shape, bf16),
                        pltpu.VMEM((nb, npos * nkv // slabs, 128), f32), small, small),
-            in_specs=[SMEM, SMEM] + [ANY] * 6,
+            in_specs=[ANY] * 8,
             out_specs=(VMEM,) * 6,
             scratch_shapes=[
+                pltpu.SMEM((nb,), jnp.int32), pltpu.SMEM((nb,), jnp.int32),
                 pltpu.VMEM(x.shape, bf16), pltpu.VMEM((dm, dq), bf16), pltpu.VMEM((dm, dh), bf16), pltpu.VMEM((dm, dh), bf16),
                 pltpu.VMEM((nb, 8, dh), bf16), pltpu.VMEM((n, nb, 8, dh), bf16), pltpu.VMEM((nb, slabs * dh, 128), bf16),
-                dma, dma((3, wch)), dma((nb * nch,)), dma((nb * nch,)), dma((n,)), dma((n,))],
+                dma((2,)), dma, dma((3, wch)), dma((nb * nch,)), dma((nb * nch,)), dma((n,)), dma((n,))],
             compiler_params=pltpu.CompilerParams(collective_id=0, has_side_effects=True, vmem_limit_bytes=12 * MIB),
-        )(pos, lens, *(pltpu.with_memory_space_constraint(t, pltpu.HBM) for t in (x, wq, wk, wv, kc, vc)))
+        )(*(pltpu.with_memory_space_constraint(t, pltpu.HBM) for t in (pos, lens, x, wq, wk, wv, kc, vc)))
 
         part, ko, vo = pl.pallas_call(
-            functools.partial(attend, ch, slabs),
+            functools.partial(attend, ch, wide, slabs),
             name='attend',
             out_shape=(jax.ShapeDtypeStruct((n, 2, 8, dh), f32), pltpu.HBM(kc.shape, bf16), pltpu.HBM(vc.shape, bf16)),
-            in_specs=[SMEM, SMEM] + [VMEM] * 6,
+            in_specs=[ANY] * 2 + [VMEM] * 6,
             out_specs=(VMEM, ANY, ANY),
             scratch_shapes=[
+                pltpu.SMEM((nb,), jnp.int32), pltpu.SMEM((nb,), jnp.int32),
                 pltpu.VMEM((nb, nkv, 128), f32), pltpu.VMEM((nb, nkv, 128), f32), pltpu.VMEM((nb, 128 // slabs, dh), f32),
                 pltpu.VMEM((nb, nkv, dh), bf16), pltpu.VMEM((nb, nkv, dh), bf16),
-                dma((nb * nch,)), dma((nb * nch,)), dma((2,))],
+                dma((2,)), dma((nb * nch,)), dma((nb * nch,)), dma((nb, 2))],
             compiler_params=pltpu.CompilerParams(vmem_limit_bytes=12 * MIB),
-        )(pos, lens, gat, kbuf, vbuf, sc, mrun, snew)
+        )(*(pltpu.with_memory_space_constraint(t, pltpu.HBM) for t in (pos, lens)), gat, kbuf, vbuf, sc, mrun, snew)
 
         ych = 4
         cols = wo.shape[1] // ych

time: 43.9 us -> 40.3 us (0.918)
  Pallas kernels: 41.2 us -> 38.9 us
  local copies, waits for them, and re-layouts: 1.91 us -> 0.61 us
    pallas_call x2, Pallas kernels: 31 us -> 28.1 us  [the longest x1 16.9 us: local(): pl.pallas_call(functools.partial(lookup, n, wch, ch, wide, slabs, early),...]
    unnamed x5 -> x1, local copies, waits for them, and re-layouts: 1.91 us -> 0.61 us
    pallas_call x1, Pallas kernels: 10.2 us -> 10.8 us  [local(): pl.pallas_call(functools.partial(combine, n, nb, ych), name='combine', ou...]
where the time goes in v1:
time: 40.3 us; the launch traced here: 40.2 us
  Pallas kernels  38.9 us (97%)
  between operations  0.66 us (2%)
  local copies, waits for them, and re-layouts  0.61 us (2%)
    pallas_call x1, Pallas kernels, local(): pl.pallas_call(functools.partial(lookup, n, wch, ch, wide, slabs, early),...  16.9 us
    pallas_call x1, Pallas kernels, local(): pl.pallas_call(functools.partial(attend, ch, wide, slabs), name='attend',...  11.2 us
    pallas_call x1, Pallas kernels, local(): pl.pallas_call(functools.partial(combine, n, nb, ych), name='combine', ou...  10.8 us

profile of v1, /device:TPU:0, one launch (start us, length us, event | category | flops | bytes accessed | tf_op | source)
XLA Modules:
  0.0 40.2 jit_solution(16372452380663430486)
XLA Ops:
  0.6 16.9 %lookup.1 = (bf16[8,2,8,128]{3,2,1,0:T(8,128)(2,1)S(1)}, bf16[2,32768,128]{2,1,0:T(8,128)(2,1)S(1)}, bf16[2,32768,128]{2,1,0:T(8,128)(2,1)S(1)}, f32[2,8192,128]...) custom-call(s32[2]{0:T(128)} %pos_hbm.3, s32[2]{0:T(128)} %lens_hbm.3, bf16[2,4096]{1,0:T(2,128)(2,1)} %x.1, ...), custom_call_target="tpu_custom_call" | custom-call | tf_op jit(solution)/shard_map/lookup/pallas_call | solution.py:351
  17.6 11.2 %attend.1 = (f32[8,2,8,128]{3,2,1,0:T(8,128)S(1)}, bf16[2,32768,128]{2,1,0:T(8,128)(2,1)}, bf16[2,32768,128]{2,1,0:T(8,128)(2,1)}) custom-call(s32[2]{0:T(128)} %pos_hbm.3, s32[2]{0:T(128)} %lens_hbm.3, bf16[8,2,8,128]{3,2,1,0:T(8,128)(2,1)S(1)} %get-tuple-element.12.gat, bf16[2,32768,128]{2,1,0:T(8,128)(2,1)S(1)} %get-tuple-element.13.kbuf, ...), custom_call_target="tpu_custom_call" | custom-call | tf_op jit(solution)/shard_map/attend/pallas_call | solution.py:366
  28.8 10.8 %combine.1 = bf16[2,4096]{1,0:T(2,128)(2,1)S(1)} custom-call(f32[8,2,8,128]{3,2,1,0:T(8,128)S(1)} %get-tuple-element.18.part, bf16[512,4096]{1,0:T(8,128)(2,1)} %wo.1), custom_call_target="tpu_custom_call" | custom-call | tf_op jit(solution)/shard_map/combine/pallas_call | solution.py:382
  39.6 0.6 %copy.13 = bf16[2,4096]{1,0:T(2,128)(2,1)} copy(bf16[2,4096]{1,0:T(2,128)(2,1)S(1)} %combine.1) | data formatting | bytes 32768

commit v2 on v1

--- a/solution.py
+++ b/solution.py
@@ -163,8 +163,7 @@
     lax.fori_loop(0, total, landed, 0)
 
 
-def attend(ch, wide, slabs, pos_hbm, lens_hbm, gat, kbuf, vbuf, sc, mrun, snew, part, ko, vo, pos, lens, mall, lrun, orun, knew, vnew,
-           isem, ksem, vsem, nsem):
+def attend(ch, wide, slabs, pos_hbm, lens_hbm, gat, kbuf, vbuf, sc, mrun, snew, part, ko, pos, lens, mall, lrun, orun, knew, isem, ksem, nsem):
     me = lax.axis_index('sp')
     nkv, nb, _, dh = gat.shape
     npos = kbuf.shape[1] // nkv
@@ -182,14 +181,12 @@
     for cp in icps:
         cp.start()
 
-    def writes(i):
+    def write_k(i):
         b, r = i // nch, pl.ds(pl.multiple_of(i % nch * crow, crow), crow)
-        return (pltpu.make_async_copy(kbuf.at[b, r], ko.at[b, r], ksem.at[i]),
-                pltpu.make_async_copy(vbuf.at[b, r], vo.at[b, r], vsem.at[i]))
+        return pltpu.make_async_copy(kbuf.at[b, r], ko.at[b, r], ksem.at[i])
 
     def begin(i, _):
-        for cp in writes(i):
-            cp.start()
+        write_k(i).start()
         return 0
 
     lax.fori_loop(0, total, begin, 0)
@@ -199,7 +196,6 @@
     orun[...] = jnp.zeros_like(orun)
     for b in range(nb):
         knew[b] = jnp.concatenate([gf[i, b, g:g + 1] for i in range(nkv)], axis=0).astype(bf16)
-        vnew[b] = jnp.concatenate([gf[i, b, g + 1:g + 2] for i in range(nkv)], axis=0).astype(bf16)
         m = jnp.broadcast_to(mrun[b].max(0, keepdims=True), (nkv, 128))
         k = heads
         while k < 128:
@@ -240,7 +236,7 @@
         e = jnp.exp2((snew[b] - jnp.where(m == ninf, 0.0, m)) * scale)
         pad = jnp.zeros_like(e)
         e16 = jnp.concatenate([e, pad], axis=0).astype(bf16)
-        v16 = jnp.concatenate([vnew[b].astype(f32), pad], axis=0).astype(bf16)
+        v16 = jnp.concatenate([gf[i, b, g + 1:g + 2] for i in range(nkv)] + [pad], axis=0).astype(bf16)
         o = orun[b] + lax.dot_general(e16, v16, (((0,), (0,)), ((), ())), preferred_element_type=f32)[0:heads]
         l = jnp.broadcast_to((lrun[b] + e).sum(0, keepdims=True), (nkv, 128))
         k = heads
@@ -254,21 +250,18 @@
             part[i, 0, b * g:(b + 1) * g, :] = o[i * g:(i + 1) * g, :]
             part[i, 1, b * g:(b + 1) * g, :] = ml[i * g:(i + 1) * g, :]
 
-    def rows(b):
+    def row(b):
         r = pl.ds(pl.multiple_of((pos[b] - start) * nkv, nkv), nkv)
-        return (pltpu.make_async_copy(knew.at[b], ko.at[b, r], nsem.at[b, 0]),
-                pltpu.make_async_copy(vnew.at[b], vo.at[b, r], nsem.at[b, 1]))
+        return pltpu.make_async_copy(knew.at[b], ko.at[b, r], nsem.at[b])
 
     def written(i, _):
-        for cp in writes(i):
-            cp.wait()
+        write_k(i).wait()
         b = i // nch
         p = pos[b] - start - i % nch * ch
 
         @pl.when(jnp.logical_and(p >= 0, p < ch))
         def _():
-            for cp in rows(b):
-                cp.start()
+            row(b).start()
 
         return 0
 
@@ -278,11 +271,62 @@
 
         @pl.when(jnp.logical_and(p >= 0, p < npos))
         def _():
-            for cp in rows(b):
-                cp.wait()
-
-
-def combine(n, nb, ych, part, wo, y, wob, rbuf, xs, ybuf, wsem, ssem, rsem, ysem, zsem):
+            row(b).wait()
+
+
+def copy_v(ch, pos_hbm, gat, vbuf, after, vo, pos, vnew, isem, vsem, nsem):
+    del after
+    me = lax.axis_index('sp')
+    nkv, nb, _, dh = gat.shape
+    npos = vbuf.shape[1] // nkv
+    nch = npos // ch
+    total = nb * nch
+    crow = ch * nkv
+    g = gat.shape[2] // 2
+    start = me * npos
+
+    def write_v(i):
+        b, r = i // nch, pl.ds(pl.multiple_of(i % nch * crow, crow), crow)
+        return pltpu.make_async_copy(vbuf.at[b, r], vo.at[b, r], vsem.at[i])
+
+    icp = pltpu.make_async_copy(pos_hbm, pos, isem)
+    icp.start()
+
+    def begin(i, _):
+        write_v(i).start()
+        return 0
+
+    lax.fori_loop(0, total, begin, 0)
+    gf = gat[...].astype(f32)
+    for b in range(nb):
+        vnew[b] = jnp.concatenate([gf[i, b, g + 1:g + 2] for i in range(nkv)], axis=0).astype(bf16)
+    icp.wait()
+
+    def row(b):
+        r = pl.ds(pl.multiple_of((pos[b] - start) * nkv, nkv), nkv)
+        return pltpu.make_async_copy(vnew.at[b], vo.at[b, r], nsem.at[b])
+
+    def written(i, _):
+        write_v(i).wait()
+        b = i // nch
+        p = pos[b] - start - i % nch * ch
+
+        @pl.when(jnp.logical_and(p >= 0, p < ch))
+        def _():
+            row(b).start()
+
+        return 0
+
+    lax.fori_loop(0, total, written, 0)
+    for b in range(nb):
+        p = pos[b] - start
+
+        @pl.when(jnp.logical_and(p >= 0, p < npos))
+        def _():
+            row(b).wait()
+
+
+def combine(n, nb, ych, part, wo, ys, wob, rbuf, xs, mine, twin, wsem, ssem, rsem, ysem, zsem):
     me = lax.axis_index('sp')
     cols = wo.shape[1] // ych
     cps = []
@@ -319,20 +363,19 @@
     sent = []
     for c in range(ych):
         cps[c].wait()
-        ybuf[me, c] = jnp.dot(xl, wob[c], preferred_element_type=f32)[0:nb]
-        for d in range(1, n):
-            cp = pltpu.make_async_remote_copy(
-                src_ref=ybuf.at[me, c], dst_ref=ybuf.at[me, c], send_sem=ysem.at[c, d], recv_sem=zsem.at[c, d],
-                device_id={'sp': lax.rem(me + d, n)}, device_id_type=MESH)
-            cp.start()
-            sent.append(cp)
-    for cp in sent:
-        cp.wait()
+        mine[c] = jnp.dot(xl, wob[c], preferred_element_type=f32)[0:nb]
+        cp = pltpu.make_async_remote_copy(
+            src_ref=mine.at[c], dst_ref=twin.at[c], send_sem=ysem.at[c], recv_sem=zsem.at[c],
+            device_id={'sp': me + 1 - 2 * lax.rem(me, 2)}, device_id_type=MESH)
+        cp.start()
+        sent.append(cp)
     for c in range(ych):
-        t = ybuf[0, c]
-        for i in range(1, n):
-            t = t + ybuf[i, c]
-        y[:, c * cols:(c + 1) * cols] = t.astype(bf16)
+        sent[c].wait()
+        ys[:, c * cols:(c + 1) * cols] = mine[c] + twin[c]
+
+
+def add4(a, b, c, d, y):
+    y[...] = ((a[...] + b[...]) + (c[...] + d[...])).astype(bf16)
 
 
 def solution(mesh):
@@ -363,34 +406,53 @@
             compiler_params=pltpu.CompilerParams(collective_id=0, has_side_effects=True, vmem_limit_bytes=12 * MIB),
         )(*(pltpu.with_memory_space_constraint(t, pltpu.HBM) for t in (pos, lens, x, wq, wk, wv, kc, vc)))
 
-        part, ko, vo = pl.pallas_call(
+        part, ko = pl.pallas_call(
             functools.partial(attend, ch, wide, slabs),
             name='attend',
-            out_shape=(jax.ShapeDtypeStruct((n, 2, 8, dh), f32), pltpu.HBM(kc.shape, bf16), pltpu.HBM(vc.shape, bf16)),
+            out_shape=(jax.ShapeDtypeStruct((n, 2, 8, dh), f32), pltpu.HBM(kc.shape, bf16)),
             in_specs=[ANY] * 2 + [VMEM] * 6,
-            out_specs=(VMEM, ANY, ANY),
+            out_specs=(VMEM, ANY),
             scratch_shapes=[
                 pltpu.SMEM((nb,), jnp.int32), pltpu.SMEM((nb,), jnp.int32),
                 pltpu.VMEM((nb, nkv, 128), f32), pltpu.VMEM((nb, nkv, 128), f32), pltpu.VMEM((nb, 128 // slabs, dh), f32),
-                pltpu.VMEM((nb, nkv, dh), bf16), pltpu.VMEM((nb, nkv, dh), bf16),
-                dma((2,)), dma((nb * nch,)), dma((nb * nch,)), dma((nb, 2))],
+                pltpu.VMEM((nb, nkv, dh), bf16), dma((2,)), dma((nb * nch,)), dma((nb,))],
             compiler_params=pltpu.CompilerParams(vmem_limit_bytes=12 * MIB),
         )(*(pltpu.with_memory_space_constraint(t, pltpu.HBM) for t in (pos, lens)), gat, kbuf, vbuf, sc, mrun, snew)
 
         ych = 4
         cols = wo.shape[1] // ych
-        y = pl.pallas_call(
+        ys = pl.pallas_call(
             functools.partial(combine, n, nb, ych),
             name='combine',
-            out_shape=jax.ShapeDtypeStruct((nb, wo.shape[1]), bf16),
+            out_shape=jax.ShapeDtypeStruct((nb, wo.shape[1]), f32),
             in_specs=[VMEM, ANY],
             out_specs=VMEM,
             scratch_shapes=[
                 pltpu.VMEM((ych, wo.shape[0], cols), bf16), pltpu.VMEM((n, 2, 8, dh), f32), pltpu.VMEM((8, wo.shape[0]), f32),
-                pltpu.VMEM((n, ych, nb, cols), f32),
-                dma((ych,)), dma((n,)), dma((n,)), dma((ych, n)), dma((ych, n))],
-            compiler_params=pltpu.CompilerParams(collective_id=1, has_side_effects=True, vmem_limit_bytes=8 * MIB),
+                pltpu.VMEM((ych, nb, cols), f32), pltpu.VMEM((ych, nb, cols), f32),
+                dma((ych,)), dma((n,)), dma((n,)), dma((ych,)), dma((ych,))],
+            compiler_params=pltpu.CompilerParams(collective_id=1, has_side_effects=True, vmem_limit_bytes=12 * MIB),
         )(part, pltpu.with_memory_space_constraint(wo, pltpu.HBM))
+        others = [lax.ppermute(ys, 'sp', [(i, i ^ d) for i in range(n)]) for d in (2, 4, 6)]
+        vo = pl.pallas_call(
+            functools.partial(copy_v, ch),
+            name='copy_v',
+            out_shape=pltpu.HBM(vc.shape, bf16),
+            in_specs=[ANY] + [VMEM] * 3,
+            out_specs=ANY,
+            scratch_shapes=[
+                pltpu.SMEM((nb,), jnp.int32), pltpu.VMEM((nb, nkv, dh), bf16), dma, dma((nb * nch,)), dma((nb,))],
+            compiler_params=pltpu.CompilerParams(vmem_limit_bytes=1 * MIB),
+            cost_estimate=pl.CostEstimate(flops=10 ** 10, bytes_accessed=24 * MIB, transcendentals=0),
+        )(pltpu.with_memory_space_constraint(pos, pltpu.HBM), gat, vbuf, ys)
+        y = pl.pallas_call(
+            add4,
+            name='add4',
+            out_shape=jax.ShapeDtypeStruct((nb, wo.shape[1]), bf16),
+            in_specs=[VMEM] * 4,
+            out_specs=VMEM,
+            compiler_params=pltpu.CompilerParams(vmem_limit_bytes=2 * MIB),
+        )(ys, *others)
         shape = (nb, npos, nkv, dh)
         return y, ko.reshape(shape), vo.reshape(shape)
 

time: 40.3 us -> 40.8 us (1.012)
  starting transfers between devices: 0 us -> 3.52 us
  Pallas kernels: 38.9 us -> 36.4 us
  local copies, waits for them, and re-layouts: 0.61 us -> 0 us
    pallas_call x0 -> x2, Pallas kernels: none -> 6.62 us  [the longest x1 5.99 us: local(): pl.pallas_call(functools.partial(copy_v, ch), name='copy_v', out_shape=pl...]
    pallas_call x1, Pallas kernels: 11.2 us -> 6.02 us  [local(): pl.pallas_call(functools.partial(attend, ch, wide, slabs), name='attend',...]
    pallas_call x1, Pallas kernels: 10.8 us -> 6.83 us  [local(): pl.pallas_call(functools.partial(combine, n, nb, ych), name='combine', ou...]
    ppermute x0 -> x3, starting transfers between devices: none -> 3.52 us  [local(): lax.ppermute(ys, 'sp', [(i, i ^ d) for i in range(n)])]
    unnamed x1 -> x0, local copies, waits for them, and re-layouts: 0.61 us -> none
  transfers between devices with their start and end apart: 0 -> 3, of which waited for: 0 -> 0; matrix products, arithmetic and copies ran while one was open for 0% -> 0% of each run, Pallas kernels for 0% -> 15%
where the time goes in v2:
time: 40.8 us; the launch traced here: 40.6 us
  Pallas kernels  36.4 us (89%)
  starting transfers between devices  3.52 us (9%)
  between operations  0.69 us (2%)
    pallas_call x1, Pallas kernels, local(): pl.pallas_call(functools.partial(lookup, n, wch, ch, wide, slabs, early),...  16.9 us
    pallas_call x1, Pallas kernels, local(): pl.pallas_call(functools.partial(combine, n, nb, ych), name='combine', ou...  6.83 us
    pallas_call x1, Pallas kernels, local(): pl.pallas_call(functools.partial(attend, ch, wide, slabs), name='attend',...  6.02 us
    pallas_call x1, Pallas kernels, local(): pl.pallas_call(functools.partial(copy_v, ch), name='copy_v', out_shape=pl...  5.99 us
    ppermute x3, starting transfers between devices, local(): lax.ppermute(ys, 'sp', [(i, i ^ d) for i in range(n)])  3.52 us
  transfers between devices with their start and end apart: 3, of which 0 were waited for; matrix products, arithmetic and copies ran while one was open for 0% of the time, Pallas kernels for 15%

profile of v2, /device:TPU:0, one launch (start us, length us, event | category | flops | bytes accessed | tf_op | source)
XLA Modules:
  0.0 40.6 jit_solution(990030137448510813)
XLA Ops:
  0.6 16.9 %lookup.1 = (bf16[8,2,8,128]{3,2,1,0:T(8,128)(2,1)S(1)}, bf16[2,32768,128]{2,1,0:T(8,128)(2,1)S(1)}, bf16[2,32768,128]{2,1,0:T(8,128)(2,1)S(1)}, f32[2,8192,128]...) custom-call(s32[2]{0:T(128)} %pos_hbm.5, s32[2]{0:T(128)} %lens_hbm.3, bf16[2,4096]{1,0:T(2,128)(2,1)} %x.1, ...), custom_call_target="tpu_custom_call" | custom-call | tf_op jit(solution)/shard_map/lookup/pallas_call | solution.py:394
  17.6 6.0 %attend.1 = (f32[8,2,8,128]{3,2,1,0:T(8,128)S(1)}, bf16[2,32768,128]{2,1,0:T(8,128)(2,1)}) custom-call(s32[2]{0:T(128)} %pos_hbm.5, s32[2]{0:T(128)} %lens_hbm.3, bf16[8,2,8,128]{3,2,1,0:T(8,128)(2,1)S(1)} %get-tuple-element.11.gat, bf16[2,32768,128]{2,1,0:T(8,128)(2,1)S(1)} %get-tuple-element.12.kbuf, bf16[2,32768,128]{2,1,0:T(8,128)(2,1)S(1)} %get-tuple-element.13.vbuf, ...), custom_call_target="tpu_custom_call" | custom-call | tf_op jit(solution)/shard_map/attend/pallas_call | solution.py:409
  23.6 6.8 %combine.1.a.after = f32[2,4096]{1,0:T(2,128)S(1)} custom-call(f32[8,2,8,128]{3,2,1,0:T(8,128)S(1)} %get-tuple-element.17.part, bf16[512,4096]{1,0:T(8,128)(2,1)} %wo.1), custom_call_target="tpu_custom_call" | custom-call | tf_op jit(solution)/shard_map/combine/pallas_call | solution.py:424
  30.4 1.5 %collective-permute-start.2 = (f32[2,4096]{1,0:T(2,128)S(1)}, f32[2,4096]{1,0:T(2,128)S(1)}, u32[]{:S(2)}, u32[]{:S(2)}) collective-permute-start(f32[2,4096]{1,0:T(2,128)S(1)} %combine.1.a.after), channel_id=1, source_target_pairs={{0,6},{1,7},{2,4},{3,5},{4,2},{5,3},{6,0},{7,1},{8,14},{9,15},{10,... | collective-permute-start | bytes 98312 | tf_op jit(solution)/shard_map/ppermute | solution.py:436
  32.0 0.7 %collective-permute-start.1 = (f32[2,4096]{1,0:T(2,128)S(1)}, f32[2,4096]{1,0:T(2,128)S(1)}, u32[]{:S(2)}, u32[]{:S(2)}) collective-permute-start(f32[2,4096]{1,0:T(2,128)S(1)} %combine.1.a.after), channel_id=1, source_target_pairs={{0,4},{1,5},{2,6},{3,7},{4,0},{5,1},{6,2},{7,3},{8,12},{9,13},{10,... | collective-permute-start | bytes 98312 | tf_op jit(solution)/shard_map/ppermute | solution.py:436
  32.7 1.3 %collective-permute-start = (f32[2,4096]{1,0:T(2,128)S(1)}, f32[2,4096]{1,0:T(2,128)S(1)}, u32[]{:S(2)}, u32[]{:S(2)}) collective-permute-start(f32[2,4096]{1,0:T(2,128)S(1)} %combine.1.a.after), channel_id=1, source_target_pairs={{0,2},{1,3},{2,0},{3,1},{4,6},{5,7},{6,4},{7,5},{8,10},{9,11},{10,... | collective-permute-start | bytes 98312 | tf_op jit(solution)/shard_map/ppermute | solution.py:436
  33.9 6.0 %copy_v.1 = bf16[2,32768,128]{2,1,0:T(8,128)(2,1)} custom-call(s32[2]{0:T(128)} %pos_hbm.5, bf16[8,2,8,128]{3,2,1,0:T(8,128)(2,1)S(1)} %get-tuple-element.11.gat, bf16[2,32768,128]{2,1,0:T(8,128)(2,1)S(1)} %get-tuple-element.13.vbuf, f32[2,4096]{1,0:T(2,128)S(1)} %combine.1.a.after), custom_call_target="tpu_custom_call" | custom-call | flops 10000000000 | bytes 25165824 | tf_op jit(solution)/shard_map/copy_v/pallas_call | solution.py:437
  39.9 0.0 collective-permute-done.2.d
  40.0 0.0 collective-permute-done.1.c
  40.0 0.0 collective-permute-done.b
  40.0 0.6 %add4.1 = bf16[2,4096]{1,0:T(2,128)(2,1)} custom-call(f32[2,4096]{1,0:T(2,128)S(1)} %combine.1.a.after, f32[2,4096]{1,0:T(2,128)S(1)} %collective-permute-done.b, f32[2,4096]{1,0:T(2,128)S(1)} %collective-permute-done.1.c, f32[2,4096]{1,0:T(2,128)S(1)} %collective-permute-done.2.d), custom_call_target="tpu_custom_call" | custom-call | tf_op jit(solution)/shard_map/add4/pallas_call | solution.py:448
Async XLA Ops:
  30.4 9.5 %collective-permute-start.2 = (f32[2,4096]{1,0:T(2,128)S(1)}, f32[2,4096]{1,0:T(2,128)S(1)}, u32[]{:S(2)}, u32[]{:S(2)}) collective-permute-start(f32[2,4096]{1,0:T(2,128)S(1)} %combine.1.a.after), channel_id=1, source_target_pairs={{0,6},{1,7},{2,4},{3,5},{4,2},{5,3},{6,0},{7,1},{8,14},{9,15},{10,... | collective-permute-start | bytes 98312 | tf_op jit(solution)/shard_map/ppermute | solution.py:436
  32.0 8.0 %collective-permute-start.1 = (f32[2,4096]{1,0:T(2,128)S(1)}, f32[2,4096]{1,0:T(2,128)S(1)}, u32[]{:S(2)}, u32[]{:S(2)}) collective-permute-start(f32[2,4096]{1,0:T(2,128)S(1)} %combine.1.a.after), channel_id=1, source_target_pairs={{0,4},{1,5},{2,6},{3,7},{4,0},{5,1},{6,2},{7,3},{8,12},{9,13},{10,... | collective-permute-start | bytes 98312 | tf_op jit(solution)/shard_map/ppermute | solution.py:436
  32.7 7.3 %collective-permute-start = (f32[2,4096]{1,0:T(2,128)S(1)}, f32[2,4096]{1,0:T(2,128)S(1)}, u32[]{:S(2)}, u32[]{:S(2)}) collective-permute-start(f32[2,4096]{1,0:T(2,128)S(1)} %combine.1.a.after), channel_id=1, source_target_pairs={{0,2},{1,3},{2,0},{3,1},{4,6},{5,7},{6,4},{7,5},{8,10},{9,11},{10,... | collective-permute-start | bytes 98312 | tf_op jit(solution)/shard_map/ppermute | solution.py:436

commit v3 on v1

--- a/solution.py
+++ b/solution.py
@@ -28,11 +28,11 @@
     pl.semaphore_wait(pltpu.get_barrier_semaphore(), n - 1)
 
 
-def lookup(n, wch, ch, wide, slabs, early, pos_hbm, lens_hbm, x, wq, wk, wv, kc, vc, gat_out, kbuf, vbuf, sc, mrun, snew,
-           pos, lens, xb, wqb, wkb, wvb, send, gat, qbd, isem, xsem, wsem, ksem, vsem, ssem, rsem):
+def lookup(n, wch, ch, wide, slabs, early, kpre, pos_hbm, lens_hbm, x, wq, wk, wv, kc, vc, gat_out, kbuf, vbuf, sc, mrun, snew,
+           pos, lens, xb, wqb, wab, send, gat, qbd, isem, xsem, wsem, ksem, vsem, ssem, rsem):
     me = lax.axis_index('sp')
     nb, dm = xb.shape
-    dq, dh = wqb.shape[1], wkb.shape[1]
+    dq, dh, da = wqb.shape[1], gat.shape[3], wab.shape[1]
     rows = dm // wch
     g = dq // dh
     nkv = n
@@ -61,32 +61,46 @@
     icps = [pltpu.make_async_copy(pos_hbm, pos, isem.at[0]), pltpu.make_async_copy(lens_hbm, lens, isem.at[1])]
     for cp in icps:
         cp.start()
-    cps = []
+    even = lax.rem(me, 2) == 0
+
+    def read_q(c):
+        r = pl.ds(c * rows, rows)
+        return pltpu.make_async_copy(wq.at[r, pl.ds(pl.multiple_of(me * dq, 128), dq)], wqb.at[r], wsem.at[0, c])
+
+    def read_a(w, c):
+        r = pl.ds(c * rows, rows)
+        return pltpu.make_async_copy(w.at[r, pl.ds(pl.multiple_of(me // 2 * da, 128), da)], wab.at[r], wsem.at[1, c])
+
     for c in range(wch):
-        r = pl.ds(c * rows, rows)
-        trio = []
-        for j, (w, buf, cols) in enumerate(((wq, wqb, dq), (wk, wkb, dh), (wv, wvb, dh))):
-            cp = pltpu.make_async_copy(w.at[r, pl.ds(pl.multiple_of(me * cols, 128), cols)], buf.at[r], wsem.at[j, c])
-            cp.start()
-            trio.append(cp)
-        cps.append(trio)
+        read_q(c).start()
+
+    @pl.when(even)
+    def _():
+        for c in range(wch):
+            read_a(wk, c).start()
+
+    @pl.when(jnp.logical_not(even))
+    def _():
+        for c in range(wch):
+            read_a(wv, c).start()
+
+    for i in range(kpre):
+        read_k(i).start()
     greet(n)
     xcp.wait()
     aq = jnp.zeros((nb, dq), f32)
-    ak = jnp.zeros((nb, dh), f32)
-    av = jnp.zeros((nb, dh), f32)
+    aa = jnp.zeros((nb, da), f32)
     for c in range(wch):
-        for cp in cps[c]:
-            cp.wait()
-        for i in range(c * total // wch, (c + 1) * total // wch):
+        read_q(c).wait()
+        read_a(wk, c).wait()
+        for i in range(kpre + c * (total - kpre) // wch, kpre + (c + 1) * (total - kpre) // wch):
             read_k(i).start()
         xc = xb[:, c * rows:(c + 1) * rows]
         r = pl.ds(c * rows, rows)
         aq += jnp.dot(xc, wqb[r, :], preferred_element_type=f32)
-        ak += jnp.dot(xc, wkb[r, :], preferred_element_type=f32)
-        av += jnp.dot(xc, wvb[r, :], preferred_element_type=f32)
-    for b in range(nb):
-        pieces = [aq[b:b + 1, i * dh:(i + 1) * dh] for i in range(g)] + [ak[b:b + 1], av[b:b + 1]]
+        aa += jnp.dot(xc, wab[r, :], preferred_element_type=f32)
+    for b in range(nb):
+        pieces = [aq[b:b + 1, i * dh:(i + 1) * dh] for i in range(g)] + [aa[b:b + 1, i * dh:(i + 1) * dh] for i in range(2)]
         pieces.append(jnp.zeros((8 - g - 2, dh), f32))
         tile = jnp.concatenate(pieces, axis=0).astype(bf16)
         send[b] = tile
@@ -117,7 +131,7 @@
     first = jnp.where(own, lane // heads * (wide // slabs), 1 << 29)
     for b in range(nb):
         q = jnp.concatenate([gf[i, b, 0:g] for i in range(nkv)], axis=0)
-        kn = jnp.concatenate([gf[i, b, g:g + 1] for i in range(nkv)], axis=0)
+        kn = jnp.concatenate([gf[i // 2 * 2, b, g + i % 2:g + i % 2 + 1] for i in range(nkv)], axis=0)
         zero = jnp.zeros_like(q)
         for s in range(slabs):
             a = jnp.concatenate([q if i == s else zero for i in range(slabs)], axis=0)
@@ -188,8 +202,8 @@
                 pltpu.make_async_copy(vbuf.at[b, r], vo.at[b, r], vsem.at[i]))
 
     def begin(i, _):
-        for cp in writes(i):
-            cp.start()
+        for t, cp in enumerate(writes(i)):
+            cp.start(priority=t)
         return 0
 
     lax.fori_loop(0, total, begin, 0)
@@ -198,8 +212,8 @@
     lrun[...] = jnp.zeros_like(lrun)
     orun[...] = jnp.zeros_like(orun)
     for b in range(nb):
-        knew[b] = jnp.concatenate([gf[i, b, g:g + 1] for i in range(nkv)], axis=0).astype(bf16)
-        vnew[b] = jnp.concatenate([gf[i, b, g + 1:g + 2] for i in range(nkv)], axis=0).astype(bf16)
+        knew[b] = jnp.concatenate([gf[i // 2 * 2, b, g + i % 2:g + i % 2 + 1] for i in range(nkv)], axis=0).astype(bf16)
+        vnew[b] = jnp.concatenate([gf[i // 2 * 2 + 1, b, g + i % 2:g + i % 2 + 1] for i in range(nkv)], axis=0).astype(bf16)
         m = jnp.broadcast_to(mrun[b].max(0, keepdims=True), (nkv, 128))
         k = heads
         while k < 128:
@@ -345,11 +359,11 @@
         dma = pltpu.SemaphoreType.DMA
         kc = kc.reshape(nb, npos * nkv, dh)
         vc = vc.reshape(nb, npos * nkv, dh)
-        wch, ch, wide, slabs, early = 8, 512, 1024, 4, 8
+        wch, ch, wide, slabs, early, kpre = 8, 512, 1024, 4, 8, 2
         nch = npos // ch
         small = jax.ShapeDtypeStruct((nb, nkv, 128), f32)
         gat, kbuf, vbuf, sc, mrun, snew = pl.pallas_call(
-            functools.partial(lookup, n, wch, ch, wide, slabs, early),
+            functools.partial(lookup, n, wch, ch, wide, slabs, early, kpre),
             name='lookup',
             out_shape=(jax.ShapeDtypeStruct((n, nb, 8, dh), bf16), pltpu.VMEM(kc.shape, bf16), pltpu.VMEM(vc.shape, bf16),
                        pltpu.VMEM((nb, npos * nkv // slabs, 128), f32), small, small),
@@ -357,9 +371,9 @@
             out_specs=(VMEM,) * 6,
             scratch_shapes=[
                 pltpu.SMEM((nb,), jnp.int32), pltpu.SMEM((nb,), jnp.int32),
-                pltpu.VMEM(x.shape, bf16), pltpu.VMEM((dm, dq), bf16), pltpu.VMEM((dm, dh), bf16), pltpu.VMEM((dm, dh), bf16),
+                pltpu.VMEM(x.shape, bf16), pltpu.VMEM((dm, dq), bf16), pltpu.VMEM((dm, 2 * dh), bf16),
                 pltpu.VMEM((nb, 8, dh), bf16), pltpu.VMEM((n, nb, 8, dh), bf16), pltpu.VMEM((nb, slabs * dh, 128), bf16),
-                dma((2,)), dma, dma((3, wch)), dma((nb * nch,)), dma((nb * nch,)), dma((n,)), dma((n,))],
+                dma((2,)), dma, dma((2, wch)), dma((nb * nch,)), dma((nb * nch,)), dma((n,)), dma((n,))],
             compiler_params=pltpu.CompilerParams(collective_id=0, has_side_effects=True, vmem_limit_bytes=12 * MIB),
         )(*(pltpu.with_memory_space_constraint(t, pltpu.HBM) for t in (pos, lens, x, wq, wk, wv, kc, vc)))
 

time: 40.3 us -> 40 us (level)
  no operation moved by 1% of the time
where the time goes in v3:
time: 40 us; the launch traced here: 39.9 us
  Pallas kernels  38.6 us (96%)
  between operations  0.66 us (2%)
  local copies, waits for them, and re-layouts  0.61 us (2%)
    pallas_call x1, Pallas kernels, local(): pl.pallas_call(functools.partial(lookup, n, wch, ch, wide, slabs, early,...  17 us
    pallas_call x1, Pallas kernels, local(): pl.pallas_call(functools.partial(attend, ch, wide, slabs), name='attend',...  11.2 us
    pallas_call x1, Pallas kernels, local(): pl.pallas_call(functools.partial(combine, n, nb, ych), name='combine', ou...  10.4 us

profile of v3, /device:TPU:0, one launch (start us, length us, event | category | flops | bytes accessed | tf_op | source)
XLA Modules:
  0.0 39.9 jit_solution(4805301358670379153)
XLA Ops:
  0.6 17.0 %lookup.1 = (bf16[8,2,8,128]{3,2,1,0:T(8,128)(2,1)S(1)}, bf16[2,32768,128]{2,1,0:T(8,128)(2,1)S(1)}, bf16[2,32768,128]{2,1,0:T(8,128)(2,1)S(1)}, f32[2,8192,128]...) custom-call(s32[2]{0:T(128)} %pos_hbm.3, s32[2]{0:T(128)} %lens_hbm.3, bf16[2,4096]{1,0:T(2,128)(2,1)} %x.1, ...), custom_call_target="tpu_custom_call" | custom-call | tf_op jit(solution)/shard_map/lookup/pallas_call | solution.py:365
  17.6 11.2 %attend.1 = (f32[8,2,8,128]{3,2,1,0:T(8,128)S(1)}, bf16[2,32768,128]{2,1,0:T(8,128)(2,1)}, bf16[2,32768,128]{2,1,0:T(8,128)(2,1)}) custom-call(s32[2]{0:T(128)} %pos_hbm.3, s32[2]{0:T(128)} %lens_hbm.3, bf16[8,2,8,128]{3,2,1,0:T(8,128)(2,1)S(1)} %get-tuple-element.12.gat, bf16[2,32768,128]{2,1,0:T(8,128)(2,1)S(1)} %get-tuple-element.13.kbuf, ...), custom_call_target="tpu_custom_call" | custom-call | tf_op jit(solution)/shard_map/attend/pallas_call | solution.py:380
  28.8 10.4 %combine.1 = bf16[2,4096]{1,0:T(2,128)(2,1)S(1)} custom-call(f32[8,2,8,128]{3,2,1,0:T(8,128)S(1)} %get-tuple-element.18.part, bf16[512,4096]{1,0:T(8,128)(2,1)} %wo.1), custom_call_target="tpu_custom_call" | custom-call | tf_op jit(solution)/shard_map/combine/pallas_call | solution.py:396
  39.3 0.6 %copy.13 = bf16[2,4096]{1,0:T(2,128)(2,1)} copy(bf16[2,4096]{1,0:T(2,128)(2,1)S(1)} %combine.1) | data formatting | bytes 32768

commit v4 on v3

--- a/solution.py
+++ b/solution.py
@@ -28,8 +28,8 @@
     pl.semaphore_wait(pltpu.get_barrier_semaphore(), n - 1)
 
 
-def lookup(n, wch, ch, wide, slabs, early, kpre, pos_hbm, lens_hbm, x, wq, wk, wv, kc, vc, gat_out, kbuf, vbuf, sc, mrun, snew,
-           pos, lens, xb, wqb, wab, send, gat, qbd, isem, xsem, wsem, ksem, vsem, ssem, rsem):
+def lookup(n, wch, ch, kpre, x, wq, wk, wv, kc, vc, gat_out, kbuf, vbuf,
+           xb, wqb, wab, send, gat, xsem, wsem, ksem, vsem, ssem, rsem):
     me = lax.axis_index('sp')
     nb, dm = xb.shape
     dq, dh, da = wqb.shape[1], gat.shape[3], wab.shape[1]
@@ -40,10 +40,6 @@
     nch = npos // ch
     total = nb * nch
     crow = ch * nkv
-    srow = crow // slabs
-    heads = 128 // slabs
-    start = me * npos
-    ninf = -jnp.inf
 
     def chunk(i):
         return i // nch, pl.ds(pl.multiple_of(i % nch * crow, crow), crow)
@@ -58,9 +54,6 @@
 
     xcp = pltpu.make_async_copy(x, xb, xsem)
     xcp.start()
-    icps = [pltpu.make_async_copy(pos_hbm, pos, isem.at[0]), pltpu.make_async_copy(lens_hbm, lens, isem.at[1])]
-    for cp in icps:
-        cp.start()
     even = lax.rem(me, 2) == 0
 
     def read_q(c):
@@ -105,7 +98,7 @@
         tile = jnp.concatenate(pieces, axis=0).astype(bf16)
         send[b] = tile
         gat[me, b] = tile
-    for i in range(early):
+    for i in range(total):
         read_v(i).start()
     awaited(n)
     out = []
@@ -118,66 +111,17 @@
     for cp in out:
         cp.wait()
 
-    for cp in icps:
-        cp.wait()
     gat_out[...] = gat[...]
-    gf = gat[...].astype(f32)
-    sub = lax.broadcasted_iota(jnp.int32, (nkv, 128), 0)
-    lane = lax.broadcasted_iota(jnp.int32, (nkv, 128), 1)
-    own = sub == (lane % heads) // g
-    wrow = wide * nkv // slabs
-    wch_n = npos // wide
-    per = wide // ch
-    first = jnp.where(own, lane // heads * (wide // slabs), 1 << 29)
-    for b in range(nb):
-        q = jnp.concatenate([gf[i, b, 0:g] for i in range(nkv)], axis=0)
-        kn = jnp.concatenate([gf[i // 2 * 2, b, g + i % 2:g + i % 2 + 1] for i in range(nkv)], axis=0)
-        zero = jnp.zeros_like(q)
-        for s in range(slabs):
-            a = jnp.concatenate([q if i == s else zero for i in range(slabs)], axis=0)
-            qbd[b, s * dh:(s + 1) * dh, :] = a.T.astype(bf16)
-        k16 = jnp.concatenate([kn, jnp.zeros_like(kn)], axis=0).astype(bf16)
-        t = jnp.dot(k16, qbd[b, 0:dh, :], preferred_element_type=f32)[0:nkv]
-        here = jnp.logical_and(pos[b] >= start, pos[b] < jnp.minimum(start + npos, lens[b]))
-        limit = jnp.where(here, heads, 0)
-        t = jnp.where(jnp.logical_and(own, lane < limit), t, ninf)
-        snew[b] = t
-        mrun[b] = t
-
-    def scores(i, _):
-        b, c = i // wch_n, i % wch_n
-        for t in range(per):
-            read_k(i * per + t).wait()
-
-        @pl.when(i * per + early < total)
-        def _():
-            for t in range(per):
-                read_v(i * per + t + early).start()
-
-        lim = jnp.minimum(pos[b], lens[b]) - start - c * wide
-        acc = None
-        for s in range(0, slabs, 2):
-            k2 = jnp.concatenate(
-                [kbuf[b, pl.ds(pl.multiple_of((c * slabs + s + t) * wrow, wrow), wrow), :] for t in range(2)], axis=1)
-            t = jnp.dot(k2, qbd[b, s * dh:(s + 2) * dh, :], preferred_element_type=f32)
-            acc = t if acc is None else acc + t
-        acc = acc.reshape(wrow // nkv, nkv, 128)
-        left = lim - lax.broadcasted_iota(jnp.int32, acc.shape, 0)
-        t = jnp.where(first[None] < left, acc, ninf)
-        sc[b, pl.ds(pl.multiple_of(c * wrow, wrow), wrow), :] = t.reshape(wrow, 128)
-        mrun[b] = jnp.maximum(mrun[b], t.max(0))
-        return 0
-
-    lax.fori_loop(0, nb * wch_n, scores, 0)
 
     def landed(i, _):
+        read_k(i).wait()
         read_v(i).wait()
         return 0
 
     lax.fori_loop(0, total, landed, 0)
 
 
-def attend(ch, wide, slabs, pos_hbm, lens_hbm, gat, kbuf, vbuf, sc, mrun, snew, part, ko, vo, pos, lens, mall, lrun, orun, knew, vnew,
+def attend(ch, wide, slabs, pos_hbm, lens_hbm, gat, kbuf, vbuf, part, ko, vo, pos, lens, sc, qbd, mrun, snew, mall, lrun, orun, knew, vnew,
            isem, ksem, vsem, nsem):
     me = lax.axis_index('sp')
     nkv, nb, _, dh = gat.shape
@@ -208,21 +152,62 @@
 
     lax.fori_loop(0, total, begin, 0)
 
+    wrow = wide * nkv // slabs
+    wch_n = npos // wide
     gf = gat[...].astype(f32)
     lrun[...] = jnp.zeros_like(lrun)
     orun[...] = jnp.zeros_like(orun)
-    for b in range(nb):
-        knew[b] = jnp.concatenate([gf[i // 2 * 2, b, g + i % 2:g + i % 2 + 1] for i in range(nkv)], axis=0).astype(bf16)
+    sub = lax.broadcasted_iota(jnp.int32, (nkv, 128), 0)
+    lane = lax.broadcasted_iota(jnp.int32, (nkv, 128), 1)
+    own = sub == (lane % heads) // g
+    first = jnp.where(own, lane // heads * (wide // slabs), 1 << 29)
+    for cp in icps:
+        cp.wait()
+    for b in range(nb):
+        q = jnp.concatenate([gf[i, b, 0:g] for i in range(nkv)], axis=0)
+        kn = jnp.concatenate([gf[i // 2 * 2, b, g + i % 2:g + i % 2 + 1] for i in range(nkv)], axis=0)
+        knew[b] = kn.astype(bf16)
         vnew[b] = jnp.concatenate([gf[i // 2 * 2 + 1, b, g + i % 2:g + i % 2 + 1] for i in range(nkv)], axis=0).astype(bf16)
+        zero = jnp.zeros_like(q)
+        for s in range(slabs):
+            a = jnp.concatenate([q if i == s else zero for i in range(slabs)], axis=0)
+            qbd[b, s * dh:(s + 1) * dh, :] = a.T.astype(bf16)
+        k16 = jnp.concatenate([kn, jnp.zeros_like(kn)], axis=0).astype(bf16)
+        t = jnp.dot(k16, qbd[b, 0:dh, :], preferred_element_type=f32)[0:nkv]
+        here = jnp.logical_and(pos[b] >= start, pos[b] < jnp.minimum(start + npos, lens[b]))
+        t = jnp.where(jnp.logical_and(own, lane < jnp.where(here, heads, 0)), t, ninf)
+        snew[b] = t
+        mrun[b] = t
+
+    def scores(i, _):
+        b, c = i // wch_n, i % wch_n
+        lim = jnp.minimum(pos[b], lens[b]) - start - c * wide
+
+        @pl.when(lim > 0)
+        def _():
+            acc = None
+            for s in range(0, slabs, 2):
+                k2 = jnp.concatenate(
+                    [kbuf[b, pl.ds(pl.multiple_of((c * slabs + s + t) * wrow, wrow), wrow), :] for t in range(2)], axis=1)
+                t = jnp.dot(k2, qbd[b, s * dh:(s + 2) * dh, :], preferred_element_type=f32)
+                acc = t if acc is None else acc + t
+            acc = acc.reshape(wrow // nkv, nkv, 128)
+            left = lim - lax.broadcasted_iota(jnp.int32, acc.shape, 0)
+            t = jnp.where(first[None] < left, acc, ninf)
+            sc[b, pl.ds(pl.multiple_of(c * wrow, wrow), wrow), :] = t.reshape(wrow, 128)
+            mrun[b] = jnp.maximum(mrun[b], t.max(0))
+
+        return 0
+
+    lax.fori_loop(0, nb * wch_n, scores, 0)
+
+    for b in range(nb):
         m = jnp.broadcast_to(mrun[b].max(0, keepdims=True), (nkv, 128))
         k = heads
         while k < 128:
             m = jnp.maximum(m, pltpu.roll(m, k, 1))
             k *= 2
         mall[b] = m
-
-    wrow = wide * nkv // slabs
-    wch_n = npos // wide
 
     def mix(i, _):
         b, c = i // wch_n, i % wch_n
@@ -244,8 +229,6 @@
 
         return 0
 
-    for cp in icps:
-        cp.wait()
     lax.fori_loop(0, nb * wch_n, mix, 0)
 
     half = lax.broadcasted_iota(jnp.int32, (heads, 128), 1) < 64
@@ -359,37 +342,36 @@
         dma = pltpu.SemaphoreType.DMA
         kc = kc.reshape(nb, npos * nkv, dh)
         vc = vc.reshape(nb, npos * nkv, dh)
-        wch, ch, wide, slabs, early, kpre = 8, 512, 1024, 4, 8, 2
+        wch, ch, wide, slabs, kpre = 8, 512, 1024, 4, 8
         nch = npos // ch
-        small = jax.ShapeDtypeStruct((nb, nkv, 128), f32)
-        gat, kbuf, vbuf, sc, mrun, snew = pl.pallas_call(
-            functools.partial(lookup, n, wch, ch, wide, slabs, early, kpre),
+        gat, kbuf, vbuf = pl.pallas_call(
+            functools.partial(lookup, n, wch, ch, kpre),
             name='lookup',
-            out_shape=(jax.ShapeDtypeStruct((n, nb, 8, dh), bf16), pltpu.VMEM(kc.shape, bf16), pltpu.VMEM(vc.shape, bf16),
-                       pltpu.VMEM((nb, npos * nkv // slabs, 128), f32), small, small),
-            in_specs=[ANY] * 8,
-            out_specs=(VMEM,) * 6,
+            out_shape=(jax.ShapeDtypeStruct((n, nb, 8, dh), bf16), pltpu.VMEM(kc.shape, bf16), pltpu.VMEM(vc.shape, bf16)),
+            in_specs=[ANY] * 6,
+            out_specs=(VMEM,) * 3,
             scratch_shapes=[
-                pltpu.SMEM((nb,), jnp.int32), pltpu.SMEM((nb,), jnp.int32),
                 pltpu.VMEM(x.shape, bf16), pltpu.VMEM((dm, dq), bf16), pltpu.VMEM((dm, 2 * dh), bf16),
-                pltpu.VMEM((nb, 8, dh), bf16), pltpu.VMEM((n, nb, 8, dh), bf16), pltpu.VMEM((nb, slabs * dh, 128), bf16),
-                dma((2,)), dma, dma((2, wch)), dma((nb * nch,)), dma((nb * nch,)), dma((n,)), dma((n,))],
-            compiler_params=pltpu.CompilerParams(collective_id=0, has_side_effects=True, vmem_limit_bytes=12 * MIB),
-        )(*(pltpu.with_memory_space_constraint(t, pltpu.HBM) for t in (pos, lens, x, wq, wk, wv, kc, vc)))
+                pltpu.VMEM((nb, 8, dh), bf16), pltpu.VMEM((n, nb, 8, dh), bf16),
+                dma, dma((2, wch)), dma((nb * nch,)), dma((nb * nch,)), dma((n,)), dma((n,))],
+            compiler_params=pltpu.CompilerParams(collective_id=0, has_side_effects=True, vmem_limit_bytes=25 * MIB),
+        )(*(pltpu.with_memory_space_constraint(t, pltpu.HBM) for t in (x, wq, wk, wv, kc, vc)))
 
         part, ko, vo = pl.pallas_call(
             functools.partial(attend, ch, wide, slabs),
             name='attend',
             out_shape=(jax.ShapeDtypeStruct((n, 2, 8, dh), f32), pltpu.HBM(kc.shape, bf16), pltpu.HBM(vc.shape, bf16)),
-            in_specs=[ANY] * 2 + [VMEM] * 6,
+            in_specs=[ANY] * 2 + [VMEM] * 3,
             out_specs=(VMEM, ANY, ANY),
             scratch_shapes=[
                 pltpu.SMEM((nb,), jnp.int32), pltpu.SMEM((nb,), jnp.int32),
+                pltpu.VMEM((nb, npos * nkv // slabs, 128), f32), pltpu.VMEM((nb, slabs * dh, 128), bf16),
+                pltpu.VMEM((nb, nkv, 128), f32), pltpu.VMEM((nb, nkv, 128), f32),
                 pltpu.VMEM((nb, nkv, 128), f32), pltpu.VMEM((nb, nkv, 128), f32), pltpu.VMEM((nb, 128 // slabs, dh), f32),
                 pltpu.VMEM((nb, nkv, dh), bf16), pltpu.VMEM((nb, nkv, dh), bf16),
                 dma((2,)), dma((nb * nch,)), dma((nb * nch,)), dma((nb, 2))],
-            compiler_params=pltpu.CompilerParams(vmem_limit_bytes=12 * MIB),
-        )(*(pltpu.with_memory_space_constraint(t, pltpu.HBM) for t in (pos, lens)), gat, kbuf, vbuf, sc, mrun, snew)
+            compiler_params=pltpu.CompilerParams(vmem_limit_bytes=25 * MIB),
+        )(*(pltpu.with_memory_space_constraint(t, pltpu.HBM) for t in (pos, lens)), gat, pltpu.with_memory_space_constraint(kbuf, pltpu.VMEM), pltpu.with_memory_space_constraint(vbuf, pltpu.VMEM))
 
         ych = 4
         cols = wo.shape[1] // ych

time: 40 us -> 42.9 us (1.073)
  Pallas kernels: 38.6 us -> 40.5 us
  local copies, waits for them, and re-layouts: 0.61 us -> 1.44 us
    pallas_call x1, Pallas kernels: 10.4 us -> 13.6 us  [local(): pl.pallas_call(functools.partial(combine, n, nb, ych), name='combine', ou...]
    pallas_call x1, Pallas kernels: 17 us -> 14.3 us  [local(): pl.pallas_call(functools.partial(lookup, n, wch, ch, kpre), name='lookup'...]
    pallas_call x1, Pallas kernels: 11.2 us -> 12.6 us  [local(): pl.pallas_call(functools.partial(attend, ch, wide, slabs), name='attend',...]
    unnamed x1 -> x3, local copies, waits for them, and re-layouts: 0.61 us -> 1.44 us
where the time goes in v4:
time: 42.9 us; the launch traced here: 42.6 us
  Pallas kernels  40.5 us (94%)
  local copies, waits for them, and re-layouts  1.44 us (3%)
  between operations  0.66 us (2%)
    pallas_call x1, Pallas kernels, local(): pl.pallas_call(functools.partial(lookup, n, wch, ch, kpre), name='lookup'...  14.3 us
    pallas_call x1, Pallas kernels, local(): pl.pallas_call(functools.partial(combine, n, nb, ych), name='combine', ou...  13.6 us
    pallas_call x1, Pallas kernels, local(): pl.pallas_call(functools.partial(attend, ch, wide, slabs), name='attend',...  12.6 us
    unnamed x3, local copies, waits for them, and re-layouts  1.44 us

profile of v4, /device:TPU:0, one launch (start us, length us, event | category | flops | bytes accessed | tf_op | source)
XLA Modules:
  0.0 42.6 jit_solution(13933598820593000585)
XLA Ops:
  0.6 14.3 %lookup.1 = (bf16[8,2,8,128]{3,2,1,0:T(8,128)(2,1)}, bf16[2,32768,128]{2,1,0:T(8,128)(2,1)S(1)}, bf16[2,32768,128]{2,1,0:T(8,128)(2,1)S(1)}) custom-call(bf16[2,4096]{1,0:T(2,128)(2,1)} %x.1, bf16[4096,4096]{1,0:T(8,128)(2,1)} %wq.1, bf16[4096,1024]{1,0:T(8,128)(2,1)} %wk.1, bf16[4096,1024]{1,0:T(8,128)(2,1)} %wv.1, bf16[2,32768,128]{2,1,0:T(8,128)(2,1)} %bitcast.4, ...), custom_call_target="tpu_custom_call" | custom-call | tf_op jit(solution)/shard_map/lookup/pallas_call | solution.py:347
  15.0 12.6 %attend.1 = (f32[8,2,8,128]{3,2,1,0:T(8,128)}, bf16[2,32768,128]{2,1,0:T(8,128)(2,1)}, bf16[2,32768,128]{2,1,0:T(8,128)(2,1)}) custom-call(s32[2]{0:T(128)} %pos_hbm.1, s32[2]{0:T(128)} %lens_hbm.1, bf16[8,2,8,128]{3,2,1,0:T(8,128)(2,1)} %get-tuple-element.9.gat, bf16[2,32768,128]{2,1,0:T(8,128)(2,1)S(1)} %get-tuple-element.10.kbuf, ...), custom_call_target="tpu_custom_call" | custom-call | tf_op jit(solution)/shard_map/attend/pallas_call | solution.py:360
  27.6 0.0 copy-start
  27.6 0.8 %copy-done = f32[8,2,8,128]{3,2,1,0:T(8,128)S(1)} copy-done((f32[8,2,8,128]{3,2,1,0:T(8,128)S(1)}, f32[8,2,8,128]{3,2,1,0:T(8,128)}, u32[]{:S(2)}) %copy-start) | copy-done | bytes 65560
  28.4 13.6 %combine.1 = bf16[2,4096]{1,0:T(2,128)(2,1)S(1)} custom-call(f32[8,2,8,128]{3,2,1,0:T(8,128)S(1)} %copy-done, bf16[512,4096]{1,0:T(8,128)(2,1)} %wo.1), custom_call_target="tpu_custom_call" | custom-call | tf_op jit(solution)/shard_map/combine/pallas_call | solution.py:378
  42.0 0.6 %copy.13 = bf16[2,4096]{1,0:T(2,128)(2,1)} copy(bf16[2,4096]{1,0:T(2,128)(2,1)S(1)} %combine.1) | data formatting | bytes 32768
Async XLA Ops:
  27.6 0.8 %copy-start = (f32[8,2,8,128]{3,2,1,0:T(8,128)S(1)}, f32[8,2,8,128]{3,2,1,0:T(8,128)}, u32[]{:S(2)}) copy-start(f32[8,2,8,128]{3,2,1,0:T(8,128)} %get-tuple-element.12.part) | copy-start | bytes 196612

commit v5 on v3

--- a/solution.py
+++ b/solution.py
@@ -28,8 +28,8 @@
     pl.semaphore_wait(pltpu.get_barrier_semaphore(), n - 1)
 
 
-def lookup(n, wch, ch, wide, slabs, early, kpre, pos_hbm, lens_hbm, x, wq, wk, wv, kc, vc, gat_out, kbuf, vbuf, sc, mrun, snew,
-           pos, lens, xb, wqb, wab, send, gat, qbd, isem, xsem, wsem, ksem, vsem, ssem, rsem):
+def lookup(n, wch, ch, wide, slabs, early, kpre, pos_hbm, lens_hbm, x, wq, wk, wv, kc, vc, gat_out, kbuf, vbuf, sc, mrun, snew, qbd,
+           pos, lens, xb, wqb, wab, send, gat, isem, xsem, wsem, ksem, vsem, ssem, rsem):
     me = lax.axis_index('sp')
     nb, dm = xb.shape
     dq, dh, da = wqb.shape[1], gat.shape[3], wab.shape[1]
@@ -144,15 +144,15 @@
         snew[b] = t
         mrun[b] = t
 
-    def scores(i, _):
-        b, c = i // wch_n, i % wch_n
+    def scores(c, _):
+        b = 0
         for t in range(per):
-            read_k(i * per + t).wait()
-
-        @pl.when(i * per + early < total)
+            read_k(c * per + t).wait()
+
+        @pl.when(c * per + early < total)
         def _():
             for t in range(per):
-                read_v(i * per + t + early).start()
+                read_v(c * per + t + early).start()
 
         lim = jnp.minimum(pos[b], lens[b]) - start - c * wide
         acc = None
@@ -164,11 +164,13 @@
         acc = acc.reshape(wrow // nkv, nkv, 128)
         left = lim - lax.broadcasted_iota(jnp.int32, acc.shape, 0)
         t = jnp.where(first[None] < left, acc, ninf)
-        sc[b, pl.ds(pl.multiple_of(c * wrow, wrow), wrow), :] = t.reshape(wrow, 128)
+        sc[pl.ds(pl.multiple_of(c * wrow, wrow), wrow), :] = t.reshape(wrow, 128)
         mrun[b] = jnp.maximum(mrun[b], t.max(0))
         return 0
 
-    lax.fori_loop(0, nb * wch_n, scores, 0)
+    lax.fori_loop(0, wch_n, scores, 0)
+    for i in range(nch, total):
+        read_k(i).wait()
 
     def landed(i, _):
         read_v(i).wait()
@@ -177,7 +179,7 @@
     lax.fori_loop(0, total, landed, 0)
 
 
-def attend(ch, wide, slabs, pos_hbm, lens_hbm, gat, kbuf, vbuf, sc, mrun, snew, part, ko, vo, pos, lens, mall, lrun, orun, knew, vnew,
+def attend(ch, wide, slabs, pos_hbm, lens_hbm, gat, kbuf, vbuf, sc, mrun, snew, qbd, part, ko, vo, pos, lens, rest, mall, lrun, orun, knew, vnew,
            isem, ksem, vsem, nsem):
     me = lax.axis_index('sp')
     nkv, nb, _, dh = gat.shape
@@ -214,25 +216,32 @@
     for b in range(nb):
         knew[b] = jnp.concatenate([gf[i // 2 * 2, b, g + i % 2:g + i % 2 + 1] for i in range(nkv)], axis=0).astype(bf16)
         vnew[b] = jnp.concatenate([gf[i // 2 * 2 + 1, b, g + i % 2:g + i % 2 + 1] for i in range(nkv)], axis=0).astype(bf16)
-        m = jnp.broadcast_to(mrun[b].max(0, keepdims=True), (nkv, 128))
+        mall[b] = mrun[b]
+
+    wrow = wide * nkv // slabs
+    wch_n = npos // wide
+
+    sub = lax.broadcasted_iota(jnp.int32, (nkv, 128), 0)
+    lane = lax.broadcasted_iota(jnp.int32, (nkv, 128), 1)
+    own = sub == (lane % heads) // g
+    first = jnp.where(own, lane // heads * (wide // slabs), 1 << 29)
+
+    def settle(b):
+        m = jnp.broadcast_to(mall[b].max(0, keepdims=True), (nkv, 128))
         k = heads
         while k < 128:
             m = jnp.maximum(m, pltpu.roll(m, k, 1))
             k *= 2
         mall[b] = m
 
-    wrow = wide * nkv // slabs
-    wch_n = npos // wide
-
-    def mix(i, _):
-        b, c = i // wch_n, i % wch_n
+    def mix(b, scored, c):
         lim = jnp.minimum(pos[b], lens[b]) - start - c * wide
 
         @pl.when(lim > 0)
         def _():
             m = mall[b]
             m = jnp.where(m == ninf, 0.0, m)
-            t = sc[b, pl.ds(pl.multiple_of(c * wrow, wrow), wrow), :].reshape(wrow // nkv, nkv, 128)
+            t = scored[pl.ds(pl.multiple_of(c * wrow, wrow), wrow), :].reshape(wrow // nkv, nkv, 128)
             e = jnp.exp2((t - m[None]) * scale)
             lrun[b] += e.sum(0)
             et = e.reshape(wrow, 128).astype(bf16).T
@@ -242,11 +251,38 @@
                 o += jnp.dot(et[s * heads:(s + 1) * heads], v, preferred_element_type=f32)
             orun[b] = o
 
-        return 0
+    def scores(b, scored, c):
+        lim = jnp.minimum(pos[b], lens[b]) - start - c * wide
+
+        @pl.when(lim > 0)
+        def _():
+            acc = None
+            for s in range(0, slabs, 2):
+                k2 = jnp.concatenate(
+                    [kbuf[b, pl.ds(pl.multiple_of((c * slabs + s + t) * wrow, wrow), wrow), :] for t in range(2)], axis=1)
+                t = jnp.dot(k2, qbd[b, s * dh:(s + 2) * dh, :], preferred_element_type=f32)
+                acc = t if acc is None else acc + t
+            acc = acc.reshape(wrow // nkv, nkv, 128)
+            left = lim - lax.broadcasted_iota(jnp.int32, acc.shape, 0)
+            t = jnp.where(first[None] < left, acc, ninf)
+            scored[pl.ds(pl.multiple_of(c * wrow, wrow), wrow), :] = t.reshape(wrow, 128)
+            mall[b] = jnp.maximum(mall[b], t.max(0))
+
+    def loop(step, b, scored):
+        def body(c, _):
+            step(b, scored, c)
+            return 0
+
+        lax.fori_loop(0, wch_n, body, 0)
 
     for cp in icps:
         cp.wait()
-    lax.fori_loop(0, nb * wch_n, mix, 0)
+    settle(0)
+    loop(mix, 0, sc)
+    for b in range(1, nb):
+        loop(scores, b, rest)
+        settle(b)
+        loop(mix, b, rest)
 
     half = lax.broadcasted_iota(jnp.int32, (heads, 128), 1) < 64
     for b in range(nb):
@@ -362,17 +398,18 @@
         wch, ch, wide, slabs, early, kpre = 8, 512, 1024, 4, 8, 2
         nch = npos // ch
         small = jax.ShapeDtypeStruct((nb, nkv, 128), f32)
-        gat, kbuf, vbuf, sc, mrun, snew = pl.pallas_call(
+        gat, kbuf, vbuf, sc, mrun, snew, qbd = pl.pallas_call(
             functools.partial(lookup, n, wch, ch, wide, slabs, early, kpre),
             name='lookup',
             out_shape=(jax.ShapeDtypeStruct((n, nb, 8, dh), bf16), pltpu.VMEM(kc.shape, bf16), pltpu.VMEM(vc.shape, bf16),
-                       pltpu.VMEM((nb, npos * nkv // slabs, 128), f32), small, small),
+                       pltpu.VMEM((npos * nkv // slabs, 128), f32), small, small,
+                       jax.ShapeDtypeStruct((nb, slabs * dh, 128), bf16)),
             in_specs=[ANY] * 8,
-            out_specs=(VMEM,) * 6,
+            out_specs=(VMEM,) * 7,
             scratch_shapes=[
                 pltpu.SMEM((nb,), jnp.int32), pltpu.SMEM((nb,), jnp.int32),
                 pltpu.VMEM(x.shape, bf16), pltpu.VMEM((dm, dq), bf16), pltpu.VMEM((dm, 2 * dh), bf16),
-                pltpu.VMEM((nb, 8, dh), bf16), pltpu.VMEM((n, nb, 8, dh), bf16), pltpu.VMEM((nb, slabs * dh, 128), bf16),
+                pltpu.VMEM((nb, 8, dh), bf16), pltpu.VMEM((n, nb, 8, dh), bf16),
                 dma((2,)), dma, dma((2, wch)), dma((nb * nch,)), dma((nb * nch,)), dma((n,)), dma((n,))],
             compiler_params=pltpu.CompilerParams(collective_id=0, has_side_effects=True, vmem_limit_bytes=12 * MIB),
         )(*(pltpu.with_memory_space_constraint(t, pltpu.HBM) for t in (pos, lens, x, wq, wk, wv, kc, vc)))
@@ -381,15 +418,15 @@
             functools.partial(attend, ch, wide, slabs),
             name='attend',
             out_shape=(jax.ShapeDtypeStruct((n, 2, 8, dh), f32), pltpu.HBM(kc.shape, bf16), pltpu.HBM(vc.shape, bf16)),
-            in_specs=[ANY] * 2 + [VMEM] * 6,
+            in_specs=[ANY] * 2 + [VMEM] * 7,
             out_specs=(VMEM, ANY, ANY),
             scratch_shapes=[
-                pltpu.SMEM((nb,), jnp.int32), pltpu.SMEM((nb,), jnp.int32),
+                pltpu.SMEM((nb,), jnp.int32), pltpu.SMEM((nb,), jnp.int32), pltpu.VMEM((npos * nkv // slabs, 128), f32),
                 pltpu.VMEM((nb, nkv, 128), f32), pltpu.VMEM((nb, nkv, 128), f32), pltpu.VMEM((nb, 128 // slabs, dh), f32),
                 pltpu.VMEM((nb, nkv, dh), bf16), pltpu.VMEM((nb, nkv, dh), bf16),
                 dma((2,)), dma((nb * nch,)), dma((nb * nch,)), dma((nb, 2))],
             compiler_params=pltpu.CompilerParams(vmem_limit_bytes=12 * MIB),
-        )(*(pltpu.with_memory_space_constraint(t, pltpu.HBM) for t in (pos, lens)), gat, kbuf, vbuf, sc, mrun, snew)
+        )(*(pltpu.with_memory_space_constraint(t, pltpu.HBM) for t in (pos, lens)), gat, kbuf, vbuf, sc, mrun, snew, qbd)
 
         ych = 4
         cols = wo.shape[1] // ych

time: 40 us -> 40 us (level)
    pallas_call x1, Pallas kernels: 17 us -> 15.6 us  [local(): pl.pallas_call(functools.partial(lookup, n, wch, ch, wide, slabs, early,...]
    pallas_call x1, Pallas kernels: 10.4 us -> 11.8 us  [local(): pl.pallas_call(functools.partial(combine, n, nb, ych), name='combine', ou...]
where the time goes in v5:
time: 40 us; the launch traced here: 39.9 us
  Pallas kernels  38.6 us (96%)
  between operations  0.66 us (2%)
  local copies, waits for them, and re-layouts  0.61 us (2%)
    pallas_call x1, Pallas kernels, local(): pl.pallas_call(functools.partial(lookup, n, wch, ch, wide, slabs, early,...  15.6 us
    pallas_call x1, Pallas kernels, local(): pl.pallas_call(functools.partial(combine, n, nb, ych), name='combine', ou...  11.8 us
    pallas_call x1, Pallas kernels, local(): pl.pallas_call(functools.partial(attend, ch, wide, slabs), name='attend',...  11.2 us

profile of v5, /device:TPU:0, one launch (start us, length us, event | category | flops | bytes accessed | tf_op | source)
XLA Modules:
  0.0 39.9 jit_solution(853890602279357921)
XLA Ops:
  0.6 15.6 %lookup.1 = (bf16[8,2,8,128]{3,2,1,0:T(8,128)(2,1)S(1)}, bf16[2,32768,128]{2,1,0:T(8,128)(2,1)S(1)}, bf16[2,32768,128]{2,1,0:T(8,128)(2,1)S(1)}, f32[8192,128]{1...) custom-call(s32[2]{0:T(128)} %pos_hbm.3, s32[2]{0:T(128)} %lens_hbm.3, ...), custom_call_target="tpu_custom_call" | custom-call | tf_op jit(solution)/shard_map/lookup/pallas_call | solution.py:401
  16.2 11.2 %attend.1 = (f32[8,2,8,128]{3,2,1,0:T(8,128)S(1)}, bf16[2,32768,128]{2,1,0:T(8,128)(2,1)}, bf16[2,32768,128]{2,1,0:T(8,128)(2,1)}) custom-call(s32[2]{0:T(128)} %pos_hbm.3, s32[2]{0:T(128)} %lens_hbm.3, bf16[8,2,8,128]{3,2,1,0:T(8,128)(2,1)S(1)} %get-tuple-element.13.gat, bf16[2,32768,128]{2,1,0:T(8,128)(2,1)S(1)} %get-tuple-element.14.kbuf, ...), custom_call_target="tpu_custom_call" | custom-call | tf_op jit(solution)/shard_map/attend/pallas_call | solution.py:417
  27.5 11.8 %combine.1 = bf16[2,4096]{1,0:T(2,128)(2,1)S(1)} custom-call(f32[8,2,8,128]{3,2,1,0:T(8,128)S(1)} %get-tuple-element.20.part, bf16[512,4096]{1,0:T(8,128)(2,1)} %wo.1), custom_call_target="tpu_custom_call" | custom-call | tf_op jit(solution)/shard_map/combine/pallas_call | solution.py:433
  39.3 0.6 %copy.13 = bf16[2,4096]{1,0:T(2,128)(2,1)} copy(bf16[2,4096]{1,0:T(2,128)(2,1)S(1)} %combine.1) | data formatting | bytes 32768

commit v6 on v5

--- a/solution.py
+++ b/solution.py
@@ -332,7 +332,7 @@
                 cp.wait()
 
 
-def combine(n, nb, ych, part, wo, y, wob, rbuf, xs, ybuf, wsem, ssem, rsem, ysem, zsem):
+def combine(n, nb, ych, part, wo, y, wob, rbuf, xs, mine, far, half, twin, wsem, ssem, rsem, ysem, zsem, hsem, tsem):
     me = lax.axis_index('sp')
     cols = wo.shape[1] // ych
     cps = []
@@ -366,23 +366,31 @@
         for j in range(g):
             xs[b:b + 1, j * dh:(j + 1) * dh] = out8[b * g + j:b * g + j + 1]
     xl = xs[...].astype(bf16)
+    over_x = me + 2 - 4 * lax.rem(me // 2, 2)
+    over_y = me + 4 - 8 * (me // 4)
     sent = []
     for c in range(ych):
         cps[c].wait()
-        ybuf[me, c] = jnp.dot(xl, wob[c], preferred_element_type=f32)[0:nb]
-        for d in range(1, n):
+        mine[c] = jnp.dot(xl, wob[c], preferred_element_type=f32)[0:nb]
+        for j, peer in enumerate((over_x, over_y, over_x + over_y - me)):
             cp = pltpu.make_async_remote_copy(
-                src_ref=ybuf.at[me, c], dst_ref=ybuf.at[me, c], send_sem=ysem.at[c, d], recv_sem=zsem.at[c, d],
-                device_id={'sp': lax.rem(me + d, n)}, device_id_type=MESH)
+                src_ref=mine.at[c], dst_ref=far.at[j, c], send_sem=ysem.at[c, j], recv_sem=zsem.at[c, j],
+                device_id={'sp': peer}, device_id_type=MESH)
             cp.start()
             sent.append(cp)
-    for cp in sent:
-        cp.wait()
+    swaps = []
     for c in range(ych):
-        t = ybuf[0, c]
-        for i in range(1, n):
-            t = t + ybuf[i, c]
-        y[:, c * cols:(c + 1) * cols] = t.astype(bf16)
+        for j in range(3):
+            sent[3 * c + j].wait()
+        half[c] = (mine[c] + far[0, c]) + (far[1, c] + far[2, c])
+        cp = pltpu.make_async_remote_copy(
+            src_ref=half.at[c], dst_ref=twin.at[c], send_sem=hsem.at[c], recv_sem=tsem.at[c],
+            device_id={'sp': me + 1 - 2 * lax.rem(me, 2)}, device_id_type=MESH)
+        cp.start()
+        swaps.append(cp)
+    for c in range(ych):
+        swaps[c].wait()
+        y[:, c * cols:(c + 1) * cols] = (half[c] + twin[c]).astype(bf16)
 
 
 def solution(mesh):
@@ -395,7 +403,7 @@
         dma = pltpu.SemaphoreType.DMA
         kc = kc.reshape(nb, npos * nkv, dh)
         vc = vc.reshape(nb, npos * nkv, dh)
-        wch, ch, wide, slabs, early, kpre = 8, 512, 1024, 4, 8, 2
+        wch, ch, wide, slabs, early, kpre = 8, 1024, 1024, 4, 4, 1
         nch = npos // ch
         small = jax.ShapeDtypeStruct((nb, nkv, 128), f32)
         gat, kbuf, vbuf, sc, mrun, snew, qbd = pl.pallas_call(
@@ -438,8 +446,9 @@
             out_specs=VMEM,
             scratch_shapes=[
                 pltpu.VMEM((ych, wo.shape[0], cols), bf16), pltpu.VMEM((n, 2, 8, dh), f32), pltpu.VMEM((8, wo.shape[0]), f32),
-                pltpu.VMEM((n, ych, nb, cols), f32),
-                dma((ych,)), dma((n,)), dma((n,)), dma((ych, n)), dma((ych, n))],
+                pltpu.VMEM((ych, nb, cols), f32), pltpu.VMEM((3, ych, nb, cols), f32),
+                pltpu.VMEM((ych, nb, cols), f32), pltpu.VMEM((ych, nb, cols), f32),
+                dma((ych,)), dma((n,)), dma((n,)), dma((ych, 3)), dma((ych, 3)), dma((ych,)), dma((ych,))],
             compiler_params=pltpu.CompilerParams(collective_id=1, has_side_effects=True, vmem_limit_bytes=8 * MIB),
         )(part, pltpu.with_memory_space_constraint(wo, pltpu.HBM))
         shape = (nb, npos, nkv, dh)

time: 40 us -> 39.1 us (0.978)
  Pallas kernels: 38.6 us -> 37.7 us
    pallas_call x1, Pallas kernels: 11.8 us -> 11.4 us  [local(): pl.pallas_call(functools.partial(combine, n, nb, ych), name='combine', ou...]
    pallas_call x1, Pallas kernels: 15.6 us -> 15.2 us  [local(): pl.pallas_call(functools.partial(lookup, n, wch, ch, wide, slabs, early,...]
where the time goes in v6:
time: 39.1 us; the launch traced here: 38.9 us
  Pallas kernels  37.7 us (96%)
  between operations  0.66 us (2%)
  local copies, waits for them, and re-layouts  0.61 us (2%)
    pallas_call x1, Pallas kernels, local(): pl.pallas_call(functools.partial(lookup, n, wch, ch, wide, slabs, early,...  15.2 us
    pallas_call x1, Pallas kernels, local(): pl.pallas_call(functools.partial(combine, n, nb, ych), name='combine', ou...  11.4 us
    pallas_call x1, Pallas kernels, local(): pl.pallas_call(functools.partial(attend, ch, wide, slabs), name='attend',...  11.1 us

profile of v6, /device:TPU:0, one launch (start us, length us, event | category | flops | bytes accessed | tf_op | source)
XLA Modules:
  0.0 38.9 jit_solution(13405180634500040159)
XLA Ops:
  0.6 15.2 %lookup.1 = (bf16[8,2,8,128]{3,2,1,0:T(8,128)(2,1)S(1)}, bf16[2,32768,128]{2,1,0:T(8,128)(2,1)S(1)}, bf16[2,32768,128]{2,1,0:T(8,128)(2,1)S(1)}, f32[8192,128]{1...) custom-call(s32[2]{0:T(128)} %pos_hbm.3, s32[2]{0:T(128)} %lens_hbm.3, ...), custom_call_target="tpu_custom_call" | custom-call | tf_op jit(solution)/shard_map/lookup/pallas_call | solution.py:409
  15.8 11.1 %attend.1 = (f32[8,2,8,128]{3,2,1,0:T(8,128)S(1)}, bf16[2,32768,128]{2,1,0:T(8,128)(2,1)}, bf16[2,32768,128]{2,1,0:T(8,128)(2,1)}) custom-call(s32[2]{0:T(128)} %pos_hbm.3, s32[2]{0:T(128)} %lens_hbm.3, bf16[8,2,8,128]{3,2,1,0:T(8,128)(2,1)S(1)} %get-tuple-element.13.gat, bf16[2,32768,128]{2,1,0:T(8,128)(2,1)S(1)} %get-tuple-element.14.kbuf, ...), custom_call_target="tpu_custom_call" | custom-call | tf_op jit(solution)/shard_map/attend/pallas_call | solution.py:425
  27.0 11.4 %combine.1 = bf16[2,4096]{1,0:T(2,128)(2,1)S(1)} custom-call(f32[8,2,8,128]{3,2,1,0:T(8,128)S(1)} %get-tuple-element.20.part, bf16[512,4096]{1,0:T(8,128)(2,1)} %wo.1), custom_call_target="tpu_custom_call" | custom-call | tf_op jit(solution)/shard_map/combine/pallas_call | solution.py:441
  38.3 0.6 %copy.13 = bf16[2,4096]{1,0:T(2,128)(2,1)} copy(bf16[2,4096]{1,0:T(2,128)(2,1)S(1)} %combine.1) | data formatting | bytes 32768

commit v7 on v6

--- a/solution.py
+++ b/solution.py
@@ -403,7 +403,7 @@
         dma = pltpu.SemaphoreType.DMA
         kc = kc.reshape(nb, npos * nkv, dh)
         vc = vc.reshape(nb, npos * nkv, dh)
-        wch, ch, wide, slabs, early, kpre = 8, 1024, 1024, 4, 4, 1
+        wch, ch, wide, slabs, early, kpre = 4, 1024, 1024, 4, 4, 1
         nch = npos // ch
         small = jax.ShapeDtypeStruct((nb, nkv, 128), f32)
         gat, kbuf, vbuf, sc, mrun, snew, qbd = pl.pallas_call(
@@ -423,7 +423,7 @@
         )(*(pltpu.with_memory_space_constraint(t, pltpu.HBM) for t in (pos, lens, x, wq, wk, wv, kc, vc)))
 
         part, ko, vo = pl.pallas_call(
-            functools.partial(attend, ch, wide, slabs),
+            functools.partial(attend, 2 * ch, wide, slabs),
             name='attend',
             out_shape=(jax.ShapeDtypeStruct((n, 2, 8, dh), f32), pltpu.HBM(kc.shape, bf16), pltpu.HBM(vc.shape, bf16)),
             in_specs=[ANY] * 2 + [VMEM] * 7,

time: 39.1 us -> 39 us (level)
  no operation moved by 1% of the time
where the time goes in v7:
time: 39 us; the launch traced here: 38.9 us
  Pallas kernels  37.6 us (96%)
  between operations  0.66 us (2%)
  local copies, waits for them, and re-layouts  0.61 us (2%)
    pallas_call x1, Pallas kernels, local(): pl.pallas_call(functools.partial(lookup, n, wch, ch, wide, slabs, early,...  14.9 us
    pallas_call x1, Pallas kernels, local(): pl.pallas_call(functools.partial(combine, n, nb, ych), name='combine', ou...  11.5 us
    pallas_call x1, Pallas kernels, local(): pl.pallas_call(functools.partial(attend, 2 * ch, wide, slabs), name='atte...  11.2 us

profile of v7, /device:TPU:0, one launch (start us, length us, event | category | flops | bytes accessed | tf_op | source)
XLA Modules:
  0.0 38.9 jit_solution(8740208765411076867)
XLA Ops:
  0.6 14.9 %lookup.1 = (bf16[8,2,8,128]{3,2,1,0:T(8,128)(2,1)S(1)}, bf16[2,32768,128]{2,1,0:T(8,128)(2,1)S(1)}, bf16[2,32768,128]{2,1,0:T(8,128)(2,1)S(1)}, f32[8192,128]{1...) custom-call(s32[2]{0:T(128)} %pos_hbm.3, s32[2]{0:T(128)} %lens_hbm.3, ...), custom_call_target="tpu_custom_call" | custom-call | tf_op jit(solution)/shard_map/lookup/pallas_call | solution.py:409
  15.6 11.2 %attend.1 = (f32[8,2,8,128]{3,2,1,0:T(8,128)S(1)}, bf16[2,32768,128]{2,1,0:T(8,128)(2,1)}, bf16[2,32768,128]{2,1,0:T(8,128)(2,1)}) custom-call(s32[2]{0:T(128)} %pos_hbm.3, s32[2]{0:T(128)} %lens_hbm.3, bf16[8,2,8,128]{3,2,1,0:T(8,128)(2,1)S(1)} %get-tuple-element.13.gat, bf16[2,32768,128]{2,1,0:T(8,128)(2,1)S(1)} %get-tuple-element.14.kbuf, ...), custom_call_target="tpu_custom_call" | custom-call | tf_op jit(solution)/shard_map/attend/pallas_call | solution.py:425
  26.7 11.5 %combine.1 = bf16[2,4096]{1,0:T(2,128)(2,1)S(1)} custom-call(f32[8,2,8,128]{3,2,1,0:T(8,128)S(1)} %get-tuple-element.20.part, bf16[512,4096]{1,0:T(8,128)(2,1)} %wo.1), custom_call_target="tpu_custom_call" | custom-call | tf_op jit(solution)/shard_map/combine/pallas_call | solution.py:441
  38.3 0.6 %copy.13 = bf16[2,4096]{1,0:T(2,128)(2,1)} copy(bf16[2,4096]{1,0:T(2,128)(2,1)S(1)} %combine.1) | data formatting | bytes 32768
